TPU v7x, 512 devices: a whole 4x8x8 slice. The times are simulated.
512 devices in a mesh: ia: 16 (over y_hi, z), ja: 8 (over y_lo, core), ka: 4 (over x).
Axes of the slice: x: 4, y: 8 (y_hi: 2, y_lo: 4; y = y_hi * 4 + y_lo), z: 8, core: 2. Of those that a mesh axis runs over, the one named last changes fastest.
Arguments:
- tile_values: bfloat16 [49152, 128], P(('ia', 'ja', 'ka')), may hold values from -0.59765625 to 0.59765625
- tile_rows: int32 [49152, 128], P(('ia', 'ja', 'ka')), may hold values from 0 to 63
- tile_cols: int32 [49152, 128], P(('ia', 'ja', 'ka')), may hold values from 0 to 8191
- tile_depths: int32 [49152, 128], P(('ia', 'ja', 'ka')), may hold values from 0 to 16383
- tile_live: int32 [512, 32], P(('ia', 'ja', 'ka')), may hold values from 0 to 3, as said below
- factor_b: bfloat16 [16, 8, 8192], P(None, 'ja', ('ia', 'ka')), may hold values from -6 to 6
- factor_c: bfloat16 [16, 4, 16384], P(None, 'ka', ('ia', 'ja')), may hold values from -6 to 6
- proj: float32 [16, 256], replicated, may hold values from -0.375 to 0.375
Outputs:
- tucker_y: float32 [32768, 256], P(('ia', 'ja', 'ka'))
- gram: float32 [256, 256], replicated
- new_factor: float32 [16, 32768], P(None, ('ia', 'ja', 'ka'))
Inputs may be any that keep to these rules, and one draw needn't show every extreme that they name: tile_live[d, o] counts the live leading slots among the 3 slots that device d holds for the device at index o along ja+ka within its mode-1 block; in every draw there is an owner for which every device has all 3 slots live, and every device has some owner with all 3 slots live.
All inputs are finite; a program needn't handle non-finite values.
Results may differ from a plain program's by a relative error of at most 0.0041.
Values may be sent and summed in bfloat16 or wider, within the bound.
No kernel may reach another device: no remote copies, remote signals or barrier semaphores. Data moves between devices by JAX's collectives and lax.ppermute only.
A program may use at most 64 MiB of HBM per device.

v0:
```python
import jax
import jax.numpy as jnp
from jax import lax
from jax.sharding import Mesh
from jax.sharding import PartitionSpec as P

RANK = 16
ROWS_DEV = 64
JA = ("ja_0", "ja_1")
IA_KA = ("ia_0", "ia_1", "ka")
IA_JA = ("ia_0", "ia_1", "ja_0", "ja_1")
JA_KA = ("ja_0", "ja_1", "ka")
IA_JA_KA = ("ia_0", "ia_1", "ja_0", "ja_1", "ka")
IA = ("ia_0", "ia_1")


def from_everyone(x, axis):
    copies = jnp.broadcast_to(x, (lax.axis_size(axis), *x.shape))
    return lax.all_to_all(copies, axis, split_axis=0, concat_axis=0, tiled=True)


def in_order(parts, dim):
    parts = jnp.moveaxis(parts, 0, dim)
    dims = parts.shape
    return parts.reshape(*dims[:dim], dims[dim] * dims[dim + 1], *dims[dim + 2 :])


def collect(x, axis, dim):
    parts = from_everyone(x, axis)
    return in_order(parts, dim)


def gathered_by_axis(x, axes, dim):
    far, near = axes
    first = from_everyone(x, far)
    parts = jnp.swapaxes(from_everyone(first, near), 0, 1)
    return in_order(parts.reshape(-1, *x.shape), dim)


def owner_block(scaled, depth_rows, target):
    kron_rows = (scaled[:, None] * depth_rows[None, :]).reshape(
        scaled.shape[0] * depth_rows.shape[0], -1
    )
    onehot = (target.reshape(1, -1) == lax.iota(jnp.int32, ROWS_DEV)[:, None]).astype(jnp.bfloat16)
    return lax.dot_general(
        onehot, kron_rows, (((1,), (1,)), ((), ())), preferred_element_type=jnp.float32
    )


def group_blocks(scaled, depth_rows, target, begin_slot, pair_size, slot_count):
    rank_size = scaled.shape[0]
    tile_width = scaled.shape[2]
    scaled_part = lax.dynamic_slice_in_dim(scaled, begin_slot, pair_size * slot_count, 1)
    depth_part = lax.dynamic_slice_in_dim(depth_rows, begin_slot, pair_size * slot_count, 1)
    target_part = lax.dynamic_slice_in_dim(target, begin_slot, pair_size * slot_count, 0)
    scaled_part = scaled_part.reshape(rank_size, pair_size, slot_count, tile_width)
    depth_part = depth_part.reshape(depth_rows.shape[0], pair_size, slot_count, tile_width)
    target_part = target_part.reshape(pair_size, slot_count, tile_width)
    return jax.vmap(owner_block, in_axes=(1, 1, 0))(scaled_part, depth_part, target_part)


def owner_total(scaled, depth_rows, target, groups, slot_count):
    pair_size = 2
    columns = scaled.shape[0] * depth_rows.shape[0]
    result = jnp.zeros((ROWS_DEV, columns), jnp.float32)

    def turn(turn_index, result):
        begin_slot = turn_index * pair_size * slot_count
        blocks = group_blocks(scaled, depth_rows, target, begin_slot, pair_size, slot_count)
        return result + jnp.sum(blocks, axis=0)

    return lax.fori_loop(0, groups // pair_size, turn, result)


def on_device(tile_values, tile_rows, tile_cols, tile_depths, tile_live, factor_b, factor_c, proj):
    owners = lax.axis_size(JA) * lax.axis_size("ka")
    slot_total = tile_values.shape[0]
    slot_count = slot_total // owners
    mode_two = collect(factor_b, IA_KA, 2)[:, 0, :]
    mode_three = gathered_by_axis(factor_c, (("ia_0", "ia_1", "ja_0"), "ja_1"), 2)[:, 0, :]
    slot_index = lax.iota(jnp.int32, slot_total)
    owner_of = slot_index // slot_count
    counts = jnp.sum(
        jnp.where(owner_of[:, None] == lax.iota(jnp.int32, owners)[None, :], tile_live, 0), axis=1
    )
    is_live = slot_index % slot_count < counts
    target = jnp.where(is_live[:, None], tile_rows, ROWS_DEV)
    scaled = (
        tile_values.astype(jnp.float32)[None]
        * jnp.take(mode_two, tile_cols, axis=1).astype(jnp.float32)
    ).astype(jnp.bfloat16)
    depth_rows = jnp.take(mode_three, tile_depths, axis=1)
    payload = jnp.concatenate([scaled, depth_rows], axis=0)
    arrived, routed = (
        lax.all_to_all(payload, JA_KA, split_axis=1, concat_axis=1, tiled=True),
        lax.all_to_all(target[None], JA_KA, split_axis=1, concat_axis=1, tiled=True),
    )
    summed = owner_total(arrived[:RANK], arrived[RANK:], routed[0], owners, slot_count)
    local_gram = lax.dot_general(
        summed,
        summed,
        (((0,), (0,)), ((), ())),
        precision=lax.Precision.HIGHEST,
        preferred_element_type=jnp.float32,
    )
    gram_total = lax.psum(local_gram, IA_JA_KA)
    gram = gram_total / (ROWS_DEV * owners * lax.axis_size(IA))
    new_factor = lax.dot_general(
        proj,
        summed,
        (((1,), (1,)), ((), ())),
        precision=lax.Precision.HIGHEST,
        preferred_element_type=jnp.float32,
    )
    return (summed, gram, new_factor)


def solution(mesh):
    finer = Mesh(
        mesh.devices.reshape(2, 8, 4, 2, mesh.shape["ka"]), ("ia_0", "ia_1", "ja_0", "ja_1", "ka")
    )
    in_specs = (
        P(IA_JA_KA, None),
        P(IA_JA_KA, None),
        P(IA_JA_KA, None),
        P(IA_JA_KA, None),
        P(IA_JA_KA, None),
        P(None, JA, IA_KA),
        P(None, "ka", IA_JA),
        P(),
    )
    out_specs = (P(IA_JA_KA, None), P(), P(None, IA_JA_KA))
    return jax.shard_map(
        on_device, mesh=finer, in_specs=in_specs, out_specs=out_specs, check_vma=False
    )
```

profile of v0, /device:TPU:1, one launch (start us, length us, event | category | flops | bytes accessed | tf_op | source)
XLA Modules:
  0.0 480.1 jit_solution(4334559632361367859)
XLA Ops:
  7.2 1.4 broadcast_in_dim.88
  8.6 17.1 %all-to-all-start.2 = ((bf16[64,16,1,128]{3,1,2,0:T(8,128)(2,1)}), bf16[64,16,1,128]{3,1,2,0:T(8,128)(2,1)S(1)}, u32[]{:S(2)}, u32[]{:S(2)}) async-start(bf16[64,16,1,128]{3,1,2,0:T(8,128)(2,1)} %broadcast_in_dim.88), calls=%async_computation.2 | async-start | bytes 524288 | tf_op jit(solution)/shard_map/all_to_all | solution.py:19
  25.8 0.8 compare_and_fusion
  26.6 0.8 bitcast_clamp_fusion
  27.4 11.5 %all-to-all-done.2 = bf16[64,16,1,128]{3,1,2,0:T(8,128)(2,1)S(1)} async-done(((bf16[64,16,1,128]{3,1,2,0:T(8,128)(2,1)}), bf16[64,16,1,128]{3,1,2,0:T(8,128)(2,1)S(1)}, u32[]{:S(2)}, u32[]{:S(2)}) %all-to-all-start.2) | async-done | bytes 262176 | tf_op jit(solution)/shard_map/all_to_all | solution.py:19
  39.0 6.7 %all_to_all.28 = bf16[2,64,16,1,128]{4,2,3,1,0:T(8,128)(2,1)S(1)} all-to-all(bf16[2,64,16,1,128]{4,2,3,1,0:T(8,128)(2,1)S(1)} %broadcast_in_dim.89), channel_id=1, replica_groups=mesh['ia_0'=2,'ia_1'=8,'ja_0'=4,'ja_1'=2,'ka'=4] {'ja_1'}, dimensions={0} | all-to-all | bytes 1048576 | tf_op jit(solution)/shard_map/all_to_all | solution.py:19
  45.6 1.4 broadcast_in_dim.84
  47.1 6.0 %all-to-all-start.1 = ((bf16[64,16,1,128]{3,1,2,0:T(8,128)(2,1)}), bf16[64,16,1,128]{3,1,2,0:T(8,128)(2,1)S(1)}, u32[]{:S(2)}, u32[]{:S(2)}) async-start(bf16[64,16,1,128]{3,1,2,0:T(8,128)(2,1)} %broadcast_in_dim.84), calls=%async_computation.1 | async-start | bytes 524288 | tf_op jit(solution)/shard_map/all_to_all | solution.py:19
  53.1 0.6 convert_element_type.12
  53.8 3.1 copy.38
  56.9 35.5 %gather_fusion.1 = bf16[12288,16]{1,0:T(8,128)(2,1)S(1)} fusion(bf16[16,16384]{0,1:T(8,128)(2,1)} %bitcast.50, s32[12288]{0:T(1024)S(1)} %bitcast_clamp_fusion), kind=kCustom, calls=%fused_computation.1 | custom fusion | bytes 835584 | tf_op jit(solution)/shard_map/jit(_take)/gather | solution.py:92
  92.4 2.1 copy.39
  94.5 1.0 copy.35
  95.6 43.6 %gather_fusion = bf16[12288,16]{1,0:T(8,128)(2,1)} fusion(bf16[16,8192]{0,1:T(8,128)(2,1)S(1)} %bitcast.49, s32[12288]{0:T(1024)S(1)} %bitcast_clamp_fusion.1), kind=kCustom, calls=%fused_computation | custom fusion | bytes 835584 | tf_op jit(solution)/shard_map/jit(_take)/gather | solution.py:90
  139.2 3.1 copy.36
  142.6 1.0 pad_maximum_fusion
  143.5 7.7 %all-to-all-start.4 = ((bf16[32,96,128]{2,0,1:T(8,128)(2,1)}), bf16[32,96,128]{2,0,1:T(8,128)(2,1)S(1)}, u32[]{:S(2)}, u32[]{:S(2)}) async-start(bf16[32,96,128]{2,0,1:T(8,128)(2,1)} %pad_maximum_fusion), calls=%async_computation.4 | async-start | bytes 1572864 | tf_op jit(solution)/shard_map/all_to_all | solution.py:95
  151.4 0.7 broadcast_select_fusion
  152.1 20.7 %all-to-all-done.4 = bf16[32,96,128]{2,0,1:T(8,128)(2,1)S(1)} async-done(((bf16[32,96,128]{2,0,1:T(8,128)(2,1)}), bf16[32,96,128]{2,0,1:T(8,128)(2,1)S(1)}, u32[]{:S(2)}, u32[]{:S(2)}) %all-to-all-start.4) | async-done | bytes 786464 | tf_op jit(solution)/shard_map/all_to_all | solution.py:95
  172.8 4.6 all-to-all-start
  177.6 7.4 %all-to-all-done = s32[1,96,128]{2,0,1:T(1,128)S(1)} async-done(((s32[1,96,128]{2,0,1:T(1,128)}), s32[1,96,128]{2,0,1:T(1,128)S(1)}, u32[]{:S(2)}, u32[]{:S(2)}) %all-to-all-start) | async-done | bytes 49184 | tf_op jit(solution)/shard_map/all_to_all | solution.py:96
  185.0 15.0 %while.16 = (s32[]{:T(128)}, f32[64,256]{1,0:T(8,128)S(1)}, s32[96,128]{1,0:T(8,128)S(1)}, bf16[16,96,128]{2,0,1:T(8,128)(2,1)S(1)}, bf16[16,96,128]{2,0,1:T(8,1...) while((s32[]{:T(128)}, f32[64,256]{1,0:T(8,128)S(1)}, s32[96,128]{1,0:T(8,128)S(1)}, ...), condition=%wide.region_2.3_spmd.clone, body=%wide.region_1.2_spmd.clone.sunk | while | flops 25444360 | bytes 1965213 | solution.py:72
  185.1 0.2 broadcast_multiply_fusion.3
  185.3 0.3 mul.80
  185.6 0.3 fusion.14
  186.2 0.3 mul.80
  186.6 0.3 fusion.14
  187.1 0.3 mul.80
  187.5 0.3 fusion.14
  188.1 0.3 mul.80
  188.5 0.3 fusion.14
  188.8 0.2 broadcast_multiply_fusion.3
  189.0 0.3 mul.80
  189.4 0.3 fusion.14
  190.0 0.3 mul.80
  190.3 0.3 fusion.14
  190.9 0.3 mul.80
  191.3 0.3 fusion.14
  191.8 0.3 mul.80
  192.2 0.3 fusion.14
  192.6 0.2 broadcast_multiply_fusion.3
  192.8 0.3 mul.80
  193.2 0.3 fusion.14
  193.7 0.3 mul.80
  194.1 0.3 fusion.14
  194.5 0.2 broadcast_multiply_fusion.3
  194.7 0.3 mul.80
  195.0 0.3 fusion.14
  195.6 0.3 mul.80
  196.0 0.3 fusion.14
  196.3 0.2 broadcast_multiply_fusion.3
  196.5 0.3 mul.80
  196.9 0.3 fusion.14
  197.5 0.3 mul.80
  197.9 0.3 fusion.14
  198.2 0.2 broadcast_multiply_fusion.3
  198.4 0.3 mul.80
  198.8 0.3 fusion.14
  199.4 0.3 mul.80
  199.7 0.3 fusion.14
  200.0 1.1 fusion.5
  201.2 0.8 convolution_bitcast_fusion.1
  202.0 269.6 %all-reduce.2.cloned.1.call-done = f32[256,256]{1,0:T(8,128)} async-done(((f32[256,256]{1,0:T(8,128)}), f32[256,256]{1,0:T(8,128)}) %all-reduce.2.cloned.1.call-update) | async-done | bytes 262160 | tf_op jit(solution)/shard_map/psum | solution.py:106
  471.6 1.7 broadcast_multiply_fusion.1
  (120 shorter events, 3.6 us)
Async XLA Ops:
  7.2 194.0 %copy-start = (f32[16,256]{1,0:T(8,128)S(1)}, f32[16,256]{1,0:T(8,128)}, u32[]{:S(2)}) copy-start(f32[16,256]{1,0:T(8,128)} %param.17) | copy-start | bytes 49156
  7.2 45.9 %copy-start.4 = (s32[96,128]{1,0:T(8,128)S(1)}, s32[96,128]{1,0:T(8,128)}, u32[]{:S(2)}) copy-start(s32[96,128]{1,0:T(8,128)} %param.12) | copy-start | bytes 147460
  7.2 45.9 %copy-start.6 = (bf16[96,128]{1,0:T(8,128)(2,1)S(1)}, bf16[96,128]{1,0:T(8,128)(2,1)}, u32[]{:S(2)}) copy-start(bf16[96,128]{1,0:T(8,128)(2,1)} %param.10) | copy-start | bytes 73732
  8.6 30.2 %all-to-all-start.2 = ((bf16[64,16,1,128]{3,1,2,0:T(8,128)(2,1)}), bf16[64,16,1,128]{3,1,2,0:T(8,128)(2,1)S(1)}, u32[]{:S(2)}, u32[]{:S(2)}) async-start(bf16[64,16,1,128]{3,1,2,0:T(8,128)(2,1)} %broadcast_in_dim.88), calls=%async_computation.2 | async-start | bytes 524288 | tf_op jit(solution)/shard_map/all_to_all | solution.py:19
  47.1 47.5 %all-to-all-start.1 = ((bf16[64,16,1,128]{3,1,2,0:T(8,128)(2,1)}), bf16[64,16,1,128]{3,1,2,0:T(8,128)(2,1)S(1)}, u32[]{:S(2)}, u32[]{:S(2)}) async-start(bf16[64,16,1,128]{3,1,2,0:T(8,128)(2,1)} %broadcast_in_dim.84), calls=%async_computation.1 | async-start | bytes 524288 | tf_op jit(solution)/shard_map/all_to_all | solution.py:19
  95.6 46.7 %copy-start.2 = (bf16[96,128,16]{1,2,0:T(8,128)(2,1)S(1)}, bf16[96,128,16]{1,2,0:T(8,128)(2,1)}, u32[]{:S(2)}) copy-start(bf16[96,128,16]{1,2,0:T(8,128)(2,1)} %copy.39) | copy-start | bytes 1179652
  95.6 46.8 %copy-start.3 = (f32[96,128]{1,0:T(8,128)S(1)}, f32[96,128]{1,0:T(8,128)}, u32[]{:S(2)}) copy-start(f32[96,128]{1,0:T(8,128)} %convert_element_type.12) | copy-start | bytes 147460
  142.3 9.0 %copy-start.7 = (s32[1,32]{1,0:T(1,128)S(1)}, s32[1,32]{1,0:T(1,128)}, u32[]{:S(2)}) copy-start(s32[1,32]{1,0:T(1,128)} %param.14) | copy-start | bytes 388
  142.3 9.1 %copy-start.5 = (s32[96,128]{1,0:T(8,128)S(1)}, s32[96,128]{1,0:T(8,128)}, u32[]{:S(2)}) copy-start(s32[96,128]{1,0:T(8,128)} %param.11) | copy-start | bytes 147460
  143.5 29.3 %all-to-all-start.4 = ((bf16[32,96,128]{2,0,1:T(8,128)(2,1)}), bf16[32,96,128]{2,0,1:T(8,128)(2,1)S(1)}, u32[]{:S(2)}, u32[]{:S(2)}) async-start(bf16[32,96,128]{2,0,1:T(8,128)(2,1)} %pad_maximum_fusion), calls=%async_computation.4 | async-start | bytes 1572864 | tf_op jit(solution)/shard_map/all_to_all | solution.py:95
  172.8 12.2 %all-to-all-start = ((s32[1,96,128]{2,0,1:T(1,128)}), s32[1,96,128]{2,0,1:T(1,128)S(1)}, u32[]{:S(2)}, u32[]{:S(2)}) async-start(s32[1,96,128]{2,0,1:T(1,128)} %bitcast.1), calls=%async_computation | async-start | bytes 98304 | tf_op jit(solution)/shard_map/all_to_all | solution.py:96
  177.4 294.2 %all-reduce.2.cloned.1.call-start = ((), (), s32[]{:S(2)}) async-start(), calls=%async_computation.5 | async-start | bytes 524288 | tf_op jit(solution)/shard_map/psum | solution.py:106
  200.0 273.2 %copy-start.1 = (f32[64,256]{1,0:T(8,128)}, f32[64,256]{1,0:T(8,128)S(1)}, u32[]{:S(2)}) copy-start(f32[64,256]{1,0:T(8,128)S(1)} %get-tuple-element.132) | copy-start | bytes 196612
Sparse Core Ops, SparseCore 0:
  201.3 270.2 all-reduce.1
where the time goes:
time: 481 us; the launch traced here: 480 us
  waiting for transfers between devices  309 us (64%)
  local copies, waits for them, and re-layouts  97.9 us (20%)
  starting transfers between devices  35.5 us (7%)
  between operations  14.3 us (3%)
  other arithmetic  9.05 us (2%)
  blocking collectives  6.67 us (1%)
  matrix products  6.25 us (1%)
    psum x1, waiting for transfers between devices, on_device(): gram_total = lax.psum(local_gram, IA_JA_KA)  270 us
    gather x2, local copies, waits for them, and re-layouts, on_device(): jnp.take(mode_two, tile_cols, axis=1).astype(jnp.float32)  46.7 us
    gather x2, local copies, waits for them, and re-layouts, on_device(): depth_rows = jnp.take(mode_three, tile_depths, axis=1)  37.6 us
    all_to_all x2, starting transfers between devices, from_everyone(): return lax.all_to_all(copies, axis, split_axis=0, concat_axis=0, tiled=True)  23.1 us
    all_to_all x1, waiting for transfers between devices, on_device(): lax.all_to_all(payload, JA_KA, split_axis=1, concat_axis=1, tiled=True)  20.7 us
    all_to_all x2, waiting for transfers between devices, from_everyone(): return lax.all_to_all(copies, axis, split_axis=0, concat_axis=0, tiled=True)  11.5 us
  transfers between devices with their start and end apart: 5, of which 4 were waited for; matrix products, arithmetic and copies ran while one was open for 9% of the time, Pallas kernels for 0%

commit v1 on v0

v1 whole, which is shorter than its diff:
```python
import jax
import jax.numpy as jnp
from jax import lax
from jax.experimental import pallas as pl
from jax.experimental.pallas import tpu as pltpu
from jax.sharding import Mesh
from jax.sharding import PartitionSpec as P

RANK = 16
KR = RANK * RANK
ROWS_DEV = 64
LANES = 128
IA = ("ia",)
IA_KA = ("ia", "ka")
IA_JA = ("ia", "ja")
JA_KA = ("ja", "ka")
IA_JA_KA = ("ia", "ja", "ka")
BF16 = jnp.bfloat16
F32 = jnp.float32
VMEM = pl.BlockSpec(memory_space=pltpu.VMEM)
SMEM = pl.BlockSpec(memory_space=pltpu.SMEM)


def iota(shape, dim):
    return lax.broadcasted_iota(jnp.int32, shape, dim)


def to_everyone(x, axes):
    copies = jnp.broadcast_to(x, (lax.axis_size(axes), *x.shape))
    return lax.all_to_all(copies, axes, split_axis=0, concat_axis=0, tiled=True)


def expand_table(packed, table, picks):
    row, lane = iota((LANES, 2 * LANES), 0), iota((LANES, 2 * LANES), 1)
    for j in range(4):
        picks[j] = (((row >> 4) == 2 * j + (lane >> 7)) & ((row & 15) == (lane & 15))).astype(BF16)

    def group(g, _):
        turned = packed[pl.ds(pl.multiple_of(g * LANES, LANES), LANES), :].T
        for j in range(4):
            two = jnp.dot(turned, picks[j], preferred_element_type=F32)
            start = pl.multiple_of(g * 8 * LANES + j * 2 * LANES, 2 * LANES)
            table[pl.ds(start, LANES), :] = two[:, :LANES]
            table[pl.ds(start + LANES, LANES), :] = two[:, LANES:]
        return 0

    lax.fori_loop(0, packed.shape[0] // LANES, group, 0)


def fetch_rows(index, base, table, rows, count):
    for j in range(count):
        rows[pl.ds(j, 1), :] = table[pl.ds(index[base + j], 1), :]


def scaled_body(cols, x, packed, out, table, picks, rows0, rows1):
    expand_table(packed, table, picks)
    lane = iota((LANES, LANES), 1)

    def group(g, _):
        total = jnp.zeros((LANES, LANES), F32)
        xs = x[g].T
        for j in range(8):
            rows = (rows0, rows1)[j & 1]
            fetch_rows(cols, g * 8 * LANES + j * LANES, table, rows, LANES)
            total = jnp.where((lane >> 4) == j, rows[...] * xs[:, j : j + 1], total)
        out[g] = total.astype(BF16)
        return 0

    lax.fori_loop(0, out.shape[0], group, 0)


def partial_body(depths, scaled, target, packed, out, table, picks, rows0, rows1):
    expand_table(packed, table, picks)
    slots = target.shape[1]
    owners = out.shape[0]
    count = slots * LANES
    row, lane = iota((LANES, KR), 0), iota((LANES, KR), 1)

    def fetch(o, rows):
        fetch_rows(depths, o * count, table, rows, count)

    def compute(o, rows):
        parts = []
        hits = []
        owner_rows = target[o]
        for t in range(slots):
            tile = o * slots + t
            spread = (((row & 15) == (lane >> 4)) & ((row >> 4) == (tile & 7))).astype(BF16)
            left = jnp.dot(scaled[tile >> 3], spread, preferred_element_type=F32).astype(BF16)
            right = rows[t * LANES : (t + 1) * LANES, :].astype(BF16)
            parts.append(left * jnp.concatenate([right, right], axis=1))
            hits.append((iota((ROWS_DEV, LANES), 0) == owner_rows[t : t + 1, :]).astype(BF16))
        block = jnp.dot(
            jnp.concatenate(hits, axis=1), jnp.concatenate(parts, axis=0), preferred_element_type=F32
        )
        out[o] = block.astype(BF16)

    fetch(0, rows0)

    def pair(i, _):
        o = 2 * i
        fetch(o + 1, rows1)
        compute(o, rows0)
        fetch(jnp.minimum(o + 2, owners - 1), rows0)
        compute(o + 1, rows1)
        return 0

    lax.fori_loop(0, owners // 2, pair, 0)


def finish_body(arrived, proj, y, pieces, new_factor):
    total = arrived[0].astype(F32)
    for s in range(1, arrived.shape[0]):
        total = total + arrived[s].astype(F32)
    y[...] = total
    gram = lax.dot_general(
        total, total, (((0,), (0,)), ((), ())), precision=lax.Precision.HIGHEST, preferred_element_type=F32
    )
    pieces[...] = gram.astype(BF16)
    new_factor[...] = lax.dot_general(
        proj[...], total, (((1,), (1,)), ((), ())), precision=lax.Precision.HIGHEST, preferred_element_type=F32
    )


def scratch(positions, rows):
    return [
        pltpu.VMEM((positions, LANES), F32),
        pltpu.VMEM((4, LANES, 2 * LANES), BF16),
        pltpu.VMEM((rows, LANES), F32),
        pltpu.VMEM((rows, LANES), F32),
    ]


def cost(flops, nbytes):
    return pl.CostEstimate(flops=flops, transcendentals=0, bytes_accessed=nbytes)


def scaled_rows(cols, x, packed):
    groups = x.shape[0]
    return pl.pallas_call(
        scaled_body,
        out_shape=jax.ShapeDtypeStruct((groups, LANES, LANES), BF16),
        in_specs=[SMEM, VMEM, VMEM],
        out_specs=VMEM,
        scratch_shapes=scratch(packed.shape[0] * 8, LANES),
        cost_estimate=cost(10**9, 10**6),
        compiler_params=pltpu.CompilerParams(vmem_limit_bytes=16 * 2**20),
        name="scaled_rows",
    )(cols, x, packed)


def partial_blocks(depths, scaled, target, packed):
    owners, slots, _ = target.shape
    return pl.pallas_call(
        partial_body,
        out_shape=jax.ShapeDtypeStruct((owners, ROWS_DEV, KR), BF16),
        in_specs=[SMEM, VMEM, VMEM, VMEM],
        out_specs=VMEM,
        scratch_shapes=scratch(packed.shape[0] * 8, slots * LANES),
        cost_estimate=cost(10**9, 10**6),
        compiler_params=pltpu.CompilerParams(vmem_limit_bytes=24 * 2**20),
        name="partial_blocks",
    )(depths, scaled, target, packed)


def finish(arrived, proj):
    return pl.pallas_call(
        finish_body,
        out_shape=(
            jax.ShapeDtypeStruct((ROWS_DEV, KR), F32),
            jax.ShapeDtypeStruct((KR, KR), BF16),
            jax.ShapeDtypeStruct((RANK, ROWS_DEV), F32),
        ),
        in_specs=[VMEM, VMEM],
        out_specs=(VMEM, VMEM, VMEM),
        cost_estimate=cost(10**9, 10**6),
        compiler_params=pltpu.CompilerParams(vmem_limit_bytes=16 * 2**20),
        name="finish",
    )(arrived, proj)


def on_device(tile_values, tile_rows, tile_cols, tile_depths, tile_live, factor_b, factor_c, proj):
    owners = lax.axis_size(JA_KA)
    tiles, width = tile_values.shape
    slots = tiles // owners
    table_b = to_everyone(factor_b[:, 0, :], IA_KA).reshape(-1, LANES)
    table_c = to_everyone(factor_c[:, 0, :], IA_JA).reshape(-1, LANES)
    live = lax.iota(jnp.int32, slots)[None, :] < tile_live.reshape(owners, 1)
    target = jnp.where(live[:, :, None], tile_rows.reshape(owners, slots, width), ROWS_DEV)
    x = tile_values.astype(F32).reshape(tiles // 8, 8, width)
    scaled = scaled_rows(tile_cols.reshape(-1), x, table_b)
    blocks = partial_blocks(tile_depths.reshape(-1), scaled, target, table_c)
    arrived = lax.all_to_all(blocks, JA_KA, split_axis=0, concat_axis=0, tiled=True)
    y, gram_part, new_factor = finish(arrived, proj)
    pieces = gram_part.reshape(owners, KR // owners, KR)
    mine = jnp.sum(
        lax.all_to_all(pieces, JA_KA, split_axis=0, concat_axis=0, tiled=True).astype(F32), axis=0
    )
    mine = jnp.sum(to_everyone(mine.astype(BF16), IA).astype(F32), axis=0)
    mine = mine / (ROWS_DEV * owners * lax.axis_size(IA))
    gram = to_everyone(mine.astype(BF16), JA_KA).reshape(KR, KR).astype(F32)
    return y, gram, new_factor


def solution(mesh):
    in_specs = (
        P(IA_JA_KA, None),
        P(IA_JA_KA, None),
        P(IA_JA_KA, None),
        P(IA_JA_KA, None),
        P(IA_JA_KA, None),
        P(None, "ja", IA_KA),
        P(None, "ka", IA_JA),
        P(),
    )
    out_specs = (P(IA_JA_KA, None), P(), P(None, IA_JA_KA))
    return jax.shard_map(on_device, mesh=mesh, in_specs=in_specs, out_specs=out_specs, check_vma=False)
```

time: 481 us -> 165 us (0.34)
  waiting for transfers between devices: 309 us -> 2.88 us
  blocking collectives: 6.67 us -> 110 us
  local copies, waits for them, and re-layouts: 97.9 us -> 2.99 us
  Pallas kernels: 0 us -> 36.8 us
  starting transfers between devices: 35.5 us -> 9.2 us
  between operations: 14.3 us -> 0.76 us
  other arithmetic: 9.05 us -> 0.96 us
  matrix products: 6.25 us -> 0 us
    psum x1 -> x0, waiting for transfers between devices: 270 us -> none  [on_device(): gram_total = lax.psum(local_gram, IA_JA_KA)]
    all_to_all x1 -> x5, blocking collectives: 6.67 us -> 110 us  [the longest x3 65.8 us: to_everyone(): return lax.all_to_all(copies, axes, split_axis=0, concat_axis=0, tiled=True)]
    gather x4 -> x0, local copies, waits for them, and re-layouts: 84.3 us -> none  [the longest x2 46.7 us: on_device(): jnp.take(mode_two, tile_cols, axis=1).astype(jnp.float32)]
    pallas_call x0 -> x3, Pallas kernels: none -> 36.8 us  [the longest x1 20.6 us: partial_blocks(): pl.pallas_call(partial_body, out_shape=jax.ShapeDtypeStruct((owners, ROWS...]
    all_to_all x4 -> x1, waiting for transfers between devices: 39.6 us -> 2.88 us  [to_everyone(): return lax.all_to_all(copies, axes, split_axis=0, concat_axis=0, tiled=True)]
    all_to_all x4 -> x1, starting transfers between devices: 35.5 us -> 9.2 us  [to_everyone(): return lax.all_to_all(copies, axes, split_axis=0, concat_axis=0, tiled=True)]
    dot_general x18 -> x0, matrix products: 6.25 us -> none  [the longest x16 4.36 us: owner_block(): lax.dot_general(onehot, kron_rows, (((1,), (1,)), ((), ())), preferred_el...]
    mul x16 -> x0, local copies, waits for them, and re-layouts: 5.37 us -> none  [owner_block(): scaled[:, None] * depth_rows[None, :]]
  transfers between devices with their start and end apart: 5 -> 1, of which waited for: 4 -> 1; matrix products, arithmetic and copies ran while one was open for 9% -> 0% of each run, Pallas kernels for 0% -> 9%
where the time goes in v1:
time: 165 us; the launch traced here: 164 us
  blocking collectives  110 us (67%)
  Pallas kernels  36.8 us (22%)
  starting transfers between devices  9.2 us (6%)
  local copies, waits for them, and re-layouts  2.99 us (2%)
  waiting for transfers between devices  2.88 us (2%)
    all_to_all x3, blocking collectives, to_everyone(): return lax.all_to_all(copies, axes, split_axis=0, concat_axis=0, tiled=True)  65.8 us
    all_to_all x1, blocking collectives, on_device(): lax.all_to_all(blocks, JA_KA, split_axis=0, concat_axis=0, tiled=True)  31.2 us
    pallas_call x1, Pallas kernels, partial_blocks(): pl.pallas_call(partial_body, out_shape=jax.ShapeDtypeStruct((owners, ROWS...  20.6 us
    pallas_call x1, Pallas kernels, scaled_rows(): pl.pallas_call(scaled_body, out_shape=jax.ShapeDtypeStruct((groups, LANES...  15.1 us
    all_to_all x1, blocking collectives, on_device(): lax.all_to_all(pieces, JA_KA, split_axis=0, concat_axis=0, tiled=True)  13.4 us
    all_to_all x1, starting transfers between devices, to_everyone(): return lax.all_to_all(copies, axes, split_axis=0, concat_axis=0, tiled=True)  9.2 us
  transfers between devices with their start and end apart: 1, of which 1 were waited for; matrix products, arithmetic and copies ran while one was open for 0% of the time, Pallas kernels for 9%

profile of v1, /device:TPU:1, one launch (start us, length us, event | category | flops | bytes accessed | tf_op | source)
XLA Modules:
  0.0 164.0 jit_solution(6390717286407131877)
XLA Ops:
  0.6 0.7 broadcast_in_dim.26
  1.4 0.0 copy-start.5
  1.4 33.4 %all_to_all.30 = bf16[64,16,128]{2,1,0:T(8,128)(2,1)S(1)} all-to-all(bf16[64,16,128]{2,1,0:T(8,128)(2,1)S(1)} %broadcast_in_dim.26), channel_id=1, replica_groups=mesh['ia'=16,'ja'=8,'ka'=4] {'ia','ka'}, dimensions={0} | all-to-all | bytes 524288 | tf_op jit(solution)/shard_map/all_to_all | solution.py:30
  34.7 0.0 copy-done.5
  34.7 0.9 broadcast_in_dim.29
  35.6 0.0 copy-start.3
  35.6 9.2 %all-to-all-start.1 = ((bf16[128,16,128]{2,1,0:T(8,128)(2,1)}), bf16[128,16,128]{2,1,0:T(8,128)(2,1)S(1)}, u32[]{:S(2)}, u32[]{:S(2)}) async-start(bf16[128,16,128]{2,1,0:T(8,128)(2,1)} %broadcast_in_dim.29), calls=%async_computation.1 | async-start | bytes 1048576 | tf_op jit(solution)/shard_map/all_to_all | solution.py:30
  44.8 0.0 copy-done.3
  44.8 0.0 copy-start.4
  44.9 0.0 copy-start.6
  44.9 0.6 copy-done.6
  45.5 0.1 iota_compare_fusion
  45.6 0.0 copy-done.4
  45.6 0.0 copy-start
  45.6 0.1 broadcast_select_fusion.target
  45.7 0.7 copy-done
  46.4 0.0 copy-start.1
  46.4 15.1 %scaled_rows.1.scaled = bf16[12,128,128]{2,1,0:T(8,128)(2,1)S(1)} custom-call(s32[12288]{0:T(1024)S(1)} %bitcast.17, f32[12,8,128]{2,1,0:T(8,128)S(1)} %bitcast_convert_fusion.1.x, bf16[1024,128]{1,0:T(8,128)(2,1)S(1)} %bitcast.15), custom_call_target="tpu_custom_call" | custom-call | flops 1000000000 | bytes 1000000 | tf_op jit(solution)/shard_map/scaled_rows/pallas_call | solution.py:140
  61.5 2.9 %all-to-all-done.1 = bf16[128,16,128]{2,1,0:T(8,128)(2,1)S(1)} async-done(((bf16[128,16,128]{2,1,0:T(8,128)(2,1)}), bf16[128,16,128]{2,1,0:T(8,128)(2,1)S(1)}, u32[]{:S(2)}, u32[]{:S(2)}) %all-to-all-start.1) | async-done | bytes 524320 | tf_op jit(solution)/shard_map/all_to_all | solution.py:30
  64.4 0.0 copy-done.1
  64.4 20.6 %partial_blocks.1 = bf16[32,64,256]{2,1,0:T(8,128)(2,1)S(1)} custom-call(s32[12288]{0:T(1024)S(1)} %bitcast.18, bf16[12,128,128]{2,1,0:T(8,128)(2,1)S(1)} %scaled_rows.1.scaled, s32[32,3,128]{2,1,0:T(4,128)S(1)} %broadcast_select_fusion.target, bf16[2048,128]{1,0:T(8,128)(2,1)S(1)} %bitcast.14), custom_call_target="tpu_custom_call" | custom-call | flops 1000000000 | bytes 1000000 | tf_op jit(solution)/shard_map/partial_blocks/pallas_call | solution.py:154
  85.0 0.0 copy-start.2
  85.0 31.2 %all_to_all.31.arrived = bf16[32,64,256]{2,1,0:T(8,128)(2,1)S(1)} all-to-all(bf16[32,64,256]{2,1,0:T(8,128)(2,1)S(1)} %partial_blocks.1), channel_id=1, replica_groups=mesh['ia'=16,'ja'=8,'ka'=4] {'ja','ka'}, dimensions={0} | all-to-all | bytes 2097152 | tf_op jit(solution)/shard_map/all_to_all | solution.py:193
  116.2 0.0 copy-done.2
  116.2 1.2 finish.1
  117.4 13.4 %all_to_all.32 = bf16[32,8,256]{2,1,0:T(8,128)(2,1)S(1)} all-to-all(bf16[32,8,256]{2,1,0:T(8,128)(2,1)S(1)} %bitcast.16), channel_id=1, replica_groups=mesh['ia'=16,'ja'=8,'ka'=4] {'ja','ka'}, dimensions={0} | all-to-all | bytes 262144 | tf_op jit(solution)/shard_map/all_to_all | solution.py:197
  130.8 18.7 %all_to_all.33 = bf16[16,8,256]{2,1,0:T(8,128)(2,1)S(1)} all-to-all(bf16[16,8,256]{2,1,0:T(8,128)(2,1)S(1)} %broadcast_in_dim.30), channel_id=1, replica_groups=mesh['ia'=16,'ja'=8,'ka'=4] {'ia'}, dimensions={0} | all-to-all | bytes 131072 | tf_op jit(solution)/shard_map/all_to_all | solution.py:30
  149.6 13.7 %all_to_all.34 = bf16[32,8,256]{2,1,0:T(8,128)(2,1)S(1)} all-to-all(bf16[32,8,256]{2,1,0:T(8,128)(2,1)S(1)} %broadcast_in_dim.31), channel_id=1, replica_groups=mesh['ia'=16,'ja'=8,'ka'=4] {'ja','ka'}, dimensions={0} | all-to-all | bytes 262144 | tf_op jit(solution)/shard_map/all_to_all | solution.py:30
  163.3 0.7 bitcast_convert_fusion
  (7 shorter events, 0.1 us)
Async XLA Ops:
  1.4 33.4 %copy-start.5 = (bf16[16,1,128]{2,0,1:T(8,128)(2,1)S(1)}, bf16[16,1,128]{2,0,1:T(8,128)(2,1)}, u32[]{:S(2)}) copy-start(bf16[16,1,128]{2,0,1:T(8,128)(2,1)} %param.14) | copy-start | bytes 12292
  35.6 9.2 %copy-start.3 = (s32[96,128]{1,0:T(8,128)S(1)}, s32[96,128]{1,0:T(8,128)}, u32[]{:S(2)}) copy-start(s32[96,128]{1,0:T(8,128)} %param.9) | copy-start | bytes 147460
  35.6 28.8 %all-to-all-start.1 = ((bf16[128,16,128]{2,1,0:T(8,128)(2,1)}), bf16[128,16,128]{2,1,0:T(8,128)(2,1)S(1)}, u32[]{:S(2)}, u32[]{:S(2)}) async-start(bf16[128,16,128]{2,1,0:T(8,128)(2,1)} %broadcast_in_dim.29), calls=%async_computation.1 | async-start | bytes 1048576 | tf_op jit(solution)/shard_map/all_to_all | solution.py:30
  44.8 0.8 copy-start.4
  44.9 0.7 copy-start.6
  45.6 0.8 copy-start
  46.4 18.0 %copy-start.1 = (s32[96,128]{1,0:T(8,128)S(1)}, s32[96,128]{1,0:T(8,128)}, u32[]{:S(2)}) copy-start(s32[96,128]{1,0:T(8,128)} %param.11) | copy-start | bytes 147460
  85.0 31.2 %copy-start.2 = (f32[16,256]{1,0:T(8,128)S(1)}, f32[16,256]{1,0:T(8,128)}, u32[]{:S(2)}) copy-start(f32[16,256]{1,0:T(8,128)} %proj.1) | copy-start | bytes 49156

commit v2 on v1

v2 whole, which is shorter than its diff:
```python
import jax
import jax.numpy as jnp
from jax import lax
from jax.experimental import pallas as pl
from jax.experimental.pallas import tpu as pltpu
from jax.sharding import Mesh
from jax.sharding import PartitionSpec as P

RANK = 16
KR = RANK * RANK
ROWS_DEV = 64
LANES = 128
PACK = LANES // RANK
JA = ("yl", "co")
IA_KA = ("ia", "ka")
IA_JA = ("ia", "yl", "co")
CO_KA = ("co", "ka")
YL_KA = ("yl", "ka")
IA_JA_KA = ("ia", "yl", "co", "ka")
BF16 = jnp.bfloat16
F32 = jnp.float32
VMEM = pl.BlockSpec(memory_space=pltpu.VMEM)
SMEM = pl.BlockSpec(memory_space=pltpu.SMEM)


def iota(shape, dim):
    return lax.broadcasted_iota(jnp.int32, shape, dim)


def exchange(x, axes):
    return lax.all_to_all(x, axes, split_axis=0, concat_axis=0, tiled=True)


def to_everyone(x, axes):
    return exchange(jnp.broadcast_to(x, (lax.axis_size(axes), *x.shape)), axes)


def expand_table(ranks, table, picks):
    row, lane = iota((LANES, 2 * LANES), 0), iota((LANES, 2 * LANES), 1)
    for j in range(PACK // 2):
        picks[j] = (((row >> 4) == 2 * j + (lane >> 7)) & ((row & 15) == (lane & 15))).astype(BF16)

    def group(g, _):
        turned = ranks[pl.ds(pl.multiple_of(g * LANES, LANES), LANES), :].T
        for j in range(PACK // 2):
            two = jnp.dot(turned, picks[j], preferred_element_type=F32)
            start = pl.multiple_of((g * PACK + 2 * j) * LANES, 2 * LANES)
            table[pl.ds(start, LANES), :] = two[:, :LANES]
            table[pl.ds(start + LANES, LANES), :] = two[:, LANES:]
        return 0

    lax.fori_loop(0, ranks.shape[0] // LANES, group, 0)


def from_each(index, count):
    return [index.at[pl.ds(j, index.shape[0] - j)] for j in range(count)]


def in_turns(count, fetch, finish, rows0, rows1):
    fetch(0, rows0)

    def pair(i, _):
        o = 2 * i
        fetch(o + 1, rows1)
        finish(o, rows0)
        fetch(jnp.minimum(o + 2, count - 1), rows0)
        finish(o + 1, rows1)
        return 0

    lax.fori_loop(0, count // 2, pair, 0)


def scaled_body(cols, x, ranks, out, table, picks, rows0, rows1):
    expand_table(ranks, table, picks)
    spread = (iota((PACK, LANES), 0) == (iota((PACK, LANES), 1) >> 4)).astype(BF16)
    views = from_each(cols, PACK * LANES)

    def fetch(g, rows):
        base = g * PACK * LANES
        for j in range(PACK):
            lanes = slice(j * RANK, (j + 1) * RANK)
            for r in range(LANES):
                rows[pl.ds(r, 1), lanes] = table[pl.ds(views[j * LANES + r][base], 1), lanes]

    def finish(g, rows):
        by_lane = lax.dot_general(x[g], spread, (((0,), (0,)), ((), ())), preferred_element_type=F32)
        out[g] = (rows[...] * by_lane).astype(BF16)

    in_turns(out.shape[0], fetch, finish, rows0, rows1)


def partial_body(depths, scaled, target, ranks, out, table, picks, spreads, rows0, rows1):
    expand_table(ranks, table, picks)
    owners, slots, _ = target.shape
    count = slots * LANES
    row, lane = iota((LANES, KR), 0), iota((LANES, KR), 1)
    for j in range(PACK):
        spreads[j] = (((row & 15) == (lane >> 4)) & ((row >> 4) == j)).astype(BF16)
    views = from_each(depths, count)

    def fetch(o, rows):
        base = o * count
        for r in range(count):
            rows[pl.ds(r, 1), :] = table[pl.ds(views[r][base], 1), :]

    def finish(o, rows):
        parts = []
        hits = []
        owner_rows = target[o]
        for t in range(slots):
            tile = o * slots + t
            left = jnp.dot(scaled[tile >> 3], spreads[tile & 7], preferred_element_type=F32).astype(BF16)
            right = rows[t * LANES : (t + 1) * LANES, :].astype(BF16)
            parts.append(left * jnp.concatenate([right, right], axis=1))
            hits.append((iota((ROWS_DEV, LANES), 0) == owner_rows[t : t + 1, :]).astype(BF16))
        block = jnp.dot(
            jnp.concatenate(hits, axis=1), jnp.concatenate(parts, axis=0), preferred_element_type=F32
        )
        place = ((o >> 2) & 1) * (owners // 2) + (o >> 3) * 4 + (o & 3)
        out[place] = block.astype(BF16)

    in_turns(owners, fetch, finish, rows0, rows1)


def added(copies):
    total = copies[0].astype(F32)
    for s in range(1, copies.shape[0]):
        total = total + copies[s].astype(F32)
    return total


def finish_body(arrived, proj, y, pieces, new_factor):
    total = added(arrived)
    y[...] = total
    gram = lax.dot_general(
        total, total, (((0,), (0,)), ((), ())), precision=lax.Precision.HIGHEST, preferred_element_type=F32
    )
    pieces[...] = gram.astype(BF16).reshape(pieces.shape)
    new_factor[...] = lax.dot_general(
        proj[...], total, (((1,), (1,)), ((), ())), precision=lax.Precision.HIGHEST, preferred_element_type=F32
    )


def cost(flops, nbytes):
    return pl.CostEstimate(flops=flops, transcendentals=0, bytes_accessed=nbytes)


def call(body, name, out_shape, in_specs, args, scratch=(), limit=16, flops=10**9):
    several = isinstance(out_shape, tuple)
    return pl.pallas_call(
        body,
        out_shape=out_shape,
        in_specs=in_specs,
        out_specs=(VMEM,) * len(out_shape) if several else VMEM,
        scratch_shapes=list(scratch),
        cost_estimate=cost(flops, 10**6),
        compiler_params=pltpu.CompilerParams(vmem_limit_bytes=limit * 2**20),
        name=name,
    )(*args)


def table_scratch(ranks):
    return [pltpu.VMEM((ranks.shape[0] * PACK, LANES), F32), pltpu.VMEM((PACK // 2, LANES, 2 * LANES), BF16)]


def scaled_rows(cols, x, ranks):
    rows = pltpu.VMEM((LANES, LANES), F32)
    out = jax.ShapeDtypeStruct((x.shape[0], LANES, LANES), BF16)
    return call(
        scaled_body, "scaled_rows", out, [SMEM, VMEM, VMEM], (cols, x, ranks), [*table_scratch(ranks), rows, rows]
    )


def partial_blocks(depths, scaled, target, ranks):
    owners, slots, _ = target.shape
    rows = pltpu.VMEM((slots * LANES, LANES), F32)
    return call(
        partial_body,
        "partial_blocks",
        jax.ShapeDtypeStruct((owners, ROWS_DEV, KR), BF16),
        [SMEM, VMEM, VMEM, VMEM],
        (depths, scaled, target, ranks),
        [*table_scratch(ranks), pltpu.VMEM((PACK, LANES, KR), BF16), rows, rows],
        limit=24,
    )


def finish(arrived, proj, parts):
    out = (
        jax.ShapeDtypeStruct((ROWS_DEV, KR), F32),
        jax.ShapeDtypeStruct((parts, KR // parts, KR), BF16),
        jax.ShapeDtypeStruct((RANK, ROWS_DEV), F32),
    )
    return call(finish_body, "finish", out, [VMEM, VMEM], (arrived, proj))


def added_copies(arrived, copies, scale=None):
    def body(arrived, out):
        total = added(arrived)
        total = (total if scale is None else total * scale).astype(BF16)
        for s in range(out.shape[0]):
            out[s] = total

    out = jax.ShapeDtypeStruct((copies, *arrived.shape[1:]), BF16)
    return call(body, "added_copies", out, [VMEM], (arrived,), flops=10**7)


def halves_added(arrived):
    def body(arrived, out):
        for s in range(out.shape[0]):
            out[s] = (arrived[0, s].astype(F32) + arrived[1, s].astype(F32)).astype(BF16)

    out = jax.ShapeDtypeStruct(arrived.shape[1:], BF16)
    return call(body, "halves_added", out, [VMEM], (arrived,), flops=10**7)


def block_moved(index, parts, order):
    block, place = index >> 7, index & 127
    digits = {}
    for name, size in reversed(parts):
        digits[name] = block & (size - 1)
        block = block >> (size.bit_length() - 1)
    sizes = dict(parts)
    moved = 0
    for name in order:
        moved = moved * sizes[name] + digits[name]
    return moved * LANES + place


def on_device(tile_values, tile_rows, tile_cols, tile_depths, tile_live, factor_b, factor_c, proj):
    n_ia, n_yl, n_co, n_ka = (lax.axis_size(a) for a in ("ia", "yl", "co", "ka"))
    owners = n_yl * n_co * n_ka
    tiles, width = tile_values.shape
    slots = tiles // owners
    near = to_everyone(jnp.stack([factor_b[:, 0, :], factor_c[:, 0, :]]), "ia")
    ranks_b = to_everyone(near[:, 0], "ka").reshape(-1, LANES)
    ranks_c = to_everyone(to_everyone(near[:, 1], "yl"), "co").reshape(-1, LANES)
    cols = block_moved(tile_cols, [("ia", n_ia), ("ka", n_ka)], ["ka", "ia"])
    depths = block_moved(tile_depths, [("ia", n_ia), ("yl", n_yl), ("co", n_co)], ["co", "yl", "ia"])
    live = lax.iota(jnp.int32, slots)[None, :] < tile_live.reshape(owners, 1)
    target = jnp.where(live[:, :, None], tile_rows.reshape(owners, slots, width), ROWS_DEV)
    scaled = scaled_rows(cols.reshape(-1), tile_values.reshape(tiles // PACK, PACK, width), ranks_b)
    blocks = partial_blocks(depths.reshape(-1), scaled, target, ranks_c)
    halves = exchange(blocks, "co").reshape(n_co, owners // n_co, ROWS_DEV, KR)
    arrived = exchange(halves_added(halves), YL_KA)
    y, pieces, new_factor = finish(arrived, proj, n_co * n_ka)
    mine = added_copies(exchange(pieces, CO_KA), n_yl)
    mine = added_copies(exchange(mine, "yl"), n_ia)
    mine = added_copies(exchange(mine, "ia"), n_co * n_ka, 1.0 / (ROWS_DEV * owners * n_ia))
    gram = exchange(mine, CO_KA).reshape(KR, KR).astype(F32)
    return y, gram, new_factor


def solution(mesh):
    n_ka = mesh.shape["ka"]
    finer = Mesh(mesh.devices.reshape(-1, 4, 2, n_ka), ("ia", "yl", "co", "ka"))
    in_specs = (
        P(IA_JA_KA, None),
        P(IA_JA_KA, None),
        P(IA_JA_KA, None),
        P(IA_JA_KA, None),
        P(IA_JA_KA, None),
        P(None, JA, IA_KA),
        P(None, "ka", IA_JA),
        P(),
    )
    out_specs = (P(IA_JA_KA, None), P(), P(None, IA_JA_KA))
    return jax.shard_map(on_device, mesh=finer, in_specs=in_specs, out_specs=out_specs, check_vma=False)
```

time: 165 us -> 151 us (0.915)
  blocking collectives: 110 us -> 74.2 us
  starting transfers between devices: 9.2 us -> 24 us
  waiting for transfers between devices: 2.88 us -> 16.9 us
  Pallas kernels: 36.8 us -> 29.4 us
    all_to_all x5 -> x7, blocking collectives: 110 us -> 74.2 us  [exchange(): return lax.all_to_all(x, axes, split_axis=0, concat_axis=0, tiled=True)]
    all_to_all x1 -> x3, starting transfers between devices: 9.2 us -> 24 us  [exchange(): return lax.all_to_all(x, axes, split_axis=0, concat_axis=0, tiled=True)]
    all_to_all x1 -> x3, waiting for transfers between devices: 2.88 us -> 16.9 us  [exchange(): return lax.all_to_all(x, axes, split_axis=0, concat_axis=0, tiled=True)]
    pallas_call x3 -> x7, Pallas kernels: 36.8 us -> 29.4 us  [call(): pl.pallas_call(body, out_shape=out_shape, in_specs=in_specs, out_specs=(V...]
  transfers between devices with their start and end apart: 1 -> 3, of which waited for: 1 -> 2; matrix products, arithmetic and copies ran while one was open for 0% -> 0% of each run, Pallas kernels for 9% -> 7%
where the time goes in v2:
time: 151 us
  blocking collectives  74.2 us (49%)
  Pallas kernels  29.4 us (19%)
  starting transfers between devices  24 us (16%)
  waiting for transfers between devices  16.9 us (11%)
  local copies, waits for them, and re-layouts  3.54 us (2%)
  other arithmetic  1.66 us (1%)
    all_to_all x7, blocking collectives, exchange(): return lax.all_to_all(x, axes, split_axis=0, concat_axis=0, tiled=True)  74.2 us
    pallas_call x7, Pallas kernels, call(): pl.pallas_call(body, out_shape=out_shape, in_specs=in_specs, out_specs=(V...  29.4 us
    all_to_all x3, starting transfers between devices, exchange(): return lax.all_to_all(x, axes, split_axis=0, concat_axis=0, tiled=True)  24 us
    all_to_all x3, waiting for transfers between devices, exchange(): return lax.all_to_all(x, axes, split_axis=0, concat_axis=0, tiled=True)  16.9 us
  transfers between devices with their start and end apart: 3, of which 2 were waited for; matrix products, arithmetic and copies ran while one was open for 0% of the time, Pallas kernels for 7%

profile of v2, /device:TPU:1, one launch (start us, length us, event | category | flops | bytes accessed | tf_op | source)
XLA Modules:
  0.0 150.5 jit_solution(11581090162331057106)
XLA Ops:
  0.6 0.7 pad_maximum_fusion
  1.3 0.7 broadcast_in_dim.26
  2.0 0.0 copy-start.3
  2.0 16.4 %all-to-all-start = ((bf16[16,2,16,128]{3,2,1,0:T(8,128)(2,1)}), bf16[16,2,16,128]{3,2,1,0:T(8,128)(2,1)S(1)}, u32[]{:S(2)}, u32[]{:S(2)}) async-start(bf16[16,2,16,128]{3,2,1,0:T(8,128)(2,1)} %broadcast_in_dim.26), calls=%async_computation | async-start | bytes 262144 | tf_op jit(solution)/shard_map/all_to_all | solution.py:31
  18.4 0.0 copy-done.3
  18.4 11.4 %all-to-all-done = bf16[16,2,16,128]{3,2,1,0:T(8,128)(2,1)S(1)} async-done(((bf16[16,2,16,128]{3,2,1,0:T(8,128)(2,1)}), bf16[16,2,16,128]{3,2,1,0:T(8,128)(2,1)S(1)}, u32[]{:S(2)}, u32[]{:S(2)}) %all-to-all-start) | async-done | bytes 131104 | tf_op jit(solution)/shard_map/all_to_all | solution.py:31
  29.8 0.7 broadcast_in_dim.27
  30.6 0.0 copy-start.4
  30.6 4.1 %all-to-all-start.1 = ((bf16[4,16,16,128]{3,2,1,0:T(8,128)(2,1)}), bf16[4,16,16,128]{3,2,1,0:T(8,128)(2,1)S(1)}, u32[]{:S(2)}, u32[]{:S(2)}) async-start(bf16[4,16,16,128]{3,2,1,0:T(8,128)(2,1)} %broadcast_in_dim.27), calls=%async_computation.1 | async-start | bytes 524288 | tf_op jit(solution)/shard_map/all_to_all | solution.py:31
  34.7 0.0 copy-done.4
  34.7 5.5 %all-to-all-done.1 = bf16[4,16,16,128]{3,2,1,0:T(8,128)(2,1)S(1)} async-done(((bf16[4,16,16,128]{3,2,1,0:T(8,128)(2,1)}), bf16[4,16,16,128]{3,2,1,0:T(8,128)(2,1)S(1)}, u32[]{:S(2)}, u32[]{:S(2)}) %all-to-all-start.1) | async-done | bytes 262176 | tf_op jit(solution)/shard_map/all_to_all | solution.py:31
  40.2 0.7 broadcast_in_dim.30
  41.0 0.0 copy-start.2
  41.0 3.5 %all-to-all-start.2 = ((bf16[4,16,16,128]{3,2,1,0:T(8,128)(2,1)}), bf16[4,16,16,128]{3,2,1,0:T(8,128)(2,1)S(1)}, u32[]{:S(2)}, u32[]{:S(2)}) async-start(bf16[4,16,16,128]{3,2,1,0:T(8,128)(2,1)} %broadcast_in_dim.30), calls=%async_computation.2 | async-start | bytes 524288 | tf_op jit(solution)/shard_map/all_to_all | solution.py:31
  44.5 0.0 copy-start.5
  44.5 0.6 copy-done.5
  45.2 0.1 iota_compare_fusion
  45.2 0.0 copy-done.2
  45.3 0.0 copy-start
  45.3 0.1 broadcast_select_fusion.target
  45.4 0.6 copy-done
  46.0 10.5 %scaled_rows.1.scaled = bf16[12,128,128]{2,1,0:T(8,128)(2,1)S(1)} custom-call(s32[12288]{0:T(1024)S(1)} %add_bitcast_fusion.cols, bf16[12,8,128]{2,1,0:T(8,128)(2,1)S(1)} %bitcast.21, bf16[1024,128]{1,0:T(8,128)(2,1)S(1)} %bitcast.20), custom_call_target="tpu_custom_call" | custom-call | flops 1000000000 | bytes 1000000 | tf_op jit(solution)/shard_map/scaled_rows/pallas_call | solution.py:150
  56.6 0.0 all-to-all-done.2
  56.6 0.1 broadcast_in_dim.31
  56.7 7.2 %all_to_all.50 = bf16[2,4,16,16,128]{4,3,2,1,0:T(8,128)(2,1)S(1)} all-to-all(bf16[2,4,16,16,128]{4,3,2,1,0:T(8,128)(2,1)S(1)} %broadcast_in_dim.31), channel_id=1, replica_groups=mesh['ia'=16,'yl'=4,'co'=2,'ka'=4] {'co'}, dimensions={0} | all-to-all | bytes 1048576 | tf_op jit(solution)/shard_map/all_to_all | solution.py:31
  63.9 17.6 %partial_blocks.1 = bf16[32,64,256]{2,1,0:T(8,128)(2,1)S(1)} custom-call(s32[12288]{0:T(1024)S(1)} %add_bitcast_fusion.1.depths, bf16[12,128,128]{2,1,0:T(8,128)(2,1)S(1)} %scaled_rows.1.scaled, s32[32,3,128]{2,1,0:T(4,128)S(1)} %broadcast_select_fusion.target, bf16[2048,128]{1,0:T(8,128)(2,1)S(1)} %bitcast.19), custom_call_target="tpu_custom_call" | custom-call | flops 1000000000 | bytes 1000000 | tf_op jit(solution)/shard_map/partial_blocks/pallas_call | solution.py:150
  81.5 4.6 %all_to_all.51 = bf16[32,64,256]{2,1,0:T(8,128)(2,1)S(1)} all-to-all(bf16[32,64,256]{2,1,0:T(8,128)(2,1)S(1)} %partial_blocks.1), channel_id=1, replica_groups=mesh['ia'=16,'yl'=4,'co'=2,'ka'=4] {'co'}, dimensions={0} | all-to-all | bytes 2097152 | tf_op jit(solution)/shard_map/all_to_all | solution.py:31
  86.1 0.1 halves_added.1
  86.2 0.0 copy-start.1
  86.2 19.4 %all_to_all.52.arrived = bf16[16,64,256]{2,1,0:T(8,128)(2,1)S(1)} all-to-all(bf16[16,64,256]{2,1,0:T(8,128)(2,1)S(1)} %halves_added.1), channel_id=1, replica_groups=mesh['ia'=16,'yl'=4,'co'=2,'ka'=4] {'yl','ka'}, dimensions={0} | all-to-all | bytes 1048576 | tf_op jit(solution)/shard_map/all_to_all | solution.py:31
  105.6 0.0 copy-done.1
  105.6 1.1 finish.1
  106.7 10.3 %all_to_all.53.arrived = bf16[8,32,256]{2,1,0:T(8,128)(2,1)S(1)} all-to-all(bf16[8,32,256]{2,1,0:T(8,128)(2,1)S(1)} %get-tuple-element.7), channel_id=1, replica_groups=mesh['ia'=16,'yl'=4,'co'=2,'ka'=4] {'co','ka'}, dimensions={0} | all-to-all | bytes 262144 | tf_op jit(solution)/shard_map/all_to_all | solution.py:31
  117.1 7.2 %all_to_all.54.arrived = bf16[4,32,256]{2,1,0:T(8,128)(2,1)S(1)} all-to-all(bf16[4,32,256]{2,1,0:T(8,128)(2,1)S(1)} %added_copies.3), channel_id=1, replica_groups=mesh['ia'=16,'yl'=4,'co'=2,'ka'=4] {'yl'}, dimensions={0} | all-to-all | bytes 131072 | tf_op jit(solution)/shard_map/all_to_all | solution.py:31
  124.3 14.3 %all_to_all.55.arrived = bf16[16,32,256]{2,1,0:T(8,128)(2,1)S(1)} all-to-all(bf16[16,32,256]{2,1,0:T(8,128)(2,1)S(1)} %added_copies.4), channel_id=1, replica_groups=mesh['ia'=16,'yl'=4,'co'=2,'ka'=4] {'ia'}, dimensions={0} | all-to-all | bytes 524288 | tf_op jit(solution)/shard_map/all_to_all | solution.py:31
  138.7 11.1 %all_to_all.56 = bf16[8,32,256]{2,1,0:T(8,128)(2,1)S(1)} all-to-all(bf16[8,32,256]{2,1,0:T(8,128)(2,1)S(1)} %added_copies.5), channel_id=1, replica_groups=mesh['ia'=16,'yl'=4,'co'=2,'ka'=4] {'co','ka'}, dimensions={0} | all-to-all | bytes 262144 | tf_op jit(solution)/shard_map/all_to_all | solution.py:31
  149.8 0.7 bitcast_convert_fusion
  (7 shorter events, 0.2 us)
Async XLA Ops:
  2.0 16.4 %copy-start.3 = (s32[96,128]{1,0:T(8,128)S(1)}, s32[96,128]{1,0:T(8,128)}, u32[]{:S(2)}) copy-start(s32[96,128]{1,0:T(8,128)} %param.10) | copy-start | bytes 147460
  2.0 27.8 %all-to-all-start = ((bf16[16,2,16,128]{3,2,1,0:T(8,128)(2,1)}), bf16[16,2,16,128]{3,2,1,0:T(8,128)(2,1)S(1)}, u32[]{:S(2)}, u32[]{:S(2)}) async-start(bf16[16,2,16,128]{3,2,1,0:T(8,128)(2,1)} %broadcast_in_dim.26), calls=%async_computation | async-start | bytes 262144 | tf_op jit(solution)/shard_map/all_to_all | solution.py:31
  30.6 4.1 %copy-start.4 = (s32[96,128]{1,0:T(8,128)S(1)}, s32[96,128]{1,0:T(8,128)}, u32[]{:S(2)}) copy-start(s32[96,128]{1,0:T(8,128)} %param.11) | copy-start | bytes 147460
  30.6 9.7 %all-to-all-start.1 = ((bf16[4,16,16,128]{3,2,1,0:T(8,128)(2,1)}), bf16[4,16,16,128]{3,2,1,0:T(8,128)(2,1)S(1)}, u32[]{:S(2)}, u32[]{:S(2)}) async-start(bf16[4,16,16,128]{3,2,1,0:T(8,128)(2,1)} %broadcast_in_dim.27), calls=%async_computation.1 | async-start | bytes 524288 | tf_op jit(solution)/shard_map/all_to_all | solution.py:31
  41.0 4.3 %copy-start.2 = (s32[96,128]{1,0:T(8,128)S(1)}, s32[96,128]{1,0:T(8,128)}, u32[]{:S(2)}) copy-start(s32[96,128]{1,0:T(8,128)} %param.9) | copy-start | bytes 147460
  41.0 15.6 %all-to-all-start.2 = ((bf16[4,16,16,128]{3,2,1,0:T(8,128)(2,1)}), bf16[4,16,16,128]{3,2,1,0:T(8,128)(2,1)S(1)}, u32[]{:S(2)}, u32[]{:S(2)}) async-start(bf16[4,16,16,128]{3,2,1,0:T(8,128)(2,1)} %broadcast_in_dim.30), calls=%async_computation.2 | async-start | bytes 524288 | tf_op jit(solution)/shard_map/all_to_all | solution.py:31
  44.5 0.7 copy-start.5
  45.3 0.7 copy-start
  86.2 19.4 %copy-start.1 = (f32[16,256]{1,0:T(8,128)S(1)}, f32[16,256]{1,0:T(8,128)}, u32[]{:S(2)}) copy-start(f32[16,256]{1,0:T(8,128)} %proj.1) | copy-start | bytes 49156

commit v3 on v2

v3 whole, which is shorter than its diff:
```python
import jax
import jax.numpy as jnp
from jax import lax
from jax.experimental import pallas as pl
from jax.experimental.pallas import tpu as pltpu
from jax.sharding import Mesh
from jax.sharding import PartitionSpec as P

RANK = 16
KR = RANK * RANK
ROWS_DEV = 64
LANES = 128
PACK = LANES // RANK
JA = ("yl", "co")
IA_KA = ("yh", "z", "ka")
IA_JA = ("yh", "z", "yl", "co")
CO_KA = ("co", "ka")
YL_KA = ("yl", "ka")
YH_KA = ("yh", "ka")
Y = ("yh", "yl")
IA_JA_KA = ("yh", "z", "yl", "co", "ka")
BF16 = jnp.bfloat16
F32 = jnp.float32
VMEM = pl.BlockSpec(memory_space=pltpu.VMEM)
SMEM = pl.BlockSpec(memory_space=pltpu.SMEM)


def iota(shape, dim):
    return lax.broadcasted_iota(jnp.int32, shape, dim)


def exchange(x, axes):
    return lax.all_to_all(x, axes, split_axis=0, concat_axis=0, tiled=True)


def to_everyone(x, axes):
    return exchange(jnp.broadcast_to(x, (lax.axis_size(axes), *x.shape)), axes)


def expand_table(ranks, table, turned, picks):
    groups = turned.shape[0]
    row, lane = iota((LANES, 2 * LANES), 0), iota((LANES, 2 * LANES), 1)
    for j in range(PACK // 2):
        picks[j] = (((row >> 4) == 2 * j + (lane >> 7)) & ((row & 15) == (lane & 15))).astype(BF16)
    for g in range(groups):
        turned[g] = ranks[g * LANES : (g + 1) * LANES, :].T

    def pick(j, _):
        for g in range(groups):
            two = jnp.dot(turned[g], picks[j], preferred_element_type=F32)
            table[g, 2 * j] = two[:, :LANES]
            table[g, 2 * j + 1] = two[:, LANES:]
        return 0

    lax.fori_loop(0, PACK // 2, pick, 0)


def fetch_rows(index, table, rows):
    step = 8 * LANES
    views = [index.at[pl.ds(r, index.shape[0] - r)] for r in range(step)]

    def several(g, _):
        base = pl.multiple_of(g * step, step)
        for r in range(step):
            rows[pl.ds(base + r, 1), :] = table[pl.ds(views[r][base], 1), :]
        return 0

    lax.fori_loop(0, index.shape[0] // step, several, 0)


def b_body(cols, ranks, rows, table, turned, picks):
    expand_table(ranks, table, turned, picks)
    fetch_rows(cols, table.reshape(-1, LANES), rows)


def scaled_body(rows, x, target, out, hits):
    spread = (iota((LANES, KR), 0) == (iota((LANES, KR), 1) >> 4)).astype(BF16)
    tiles = x.shape[1]
    owners, slots, _ = target.shape

    def group(g, _):
        xs = x[g].astype(F32).T
        for j in range(tiles):
            start = pl.multiple_of((g * tiles + j) * LANES, LANES)
            scaled = (rows[pl.ds(start, LANES), :] * xs[:, j : j + 1]).astype(BF16)
            out[pl.ds(start, LANES), :] = jnp.dot(scaled, spread, preferred_element_type=F32).astype(BF16)
        return 0

    lax.fori_loop(0, x.shape[0], group, 0)

    def owner(o, _):
        owner_rows = target[o]
        for t in range(slots):
            lanes = slice(t * LANES, (t + 1) * LANES)
            hits[o, :, lanes] = (iota((ROWS_DEV, LANES), 0) == owner_rows[t : t + 1, :]).astype(BF16)
        return 0

    lax.fori_loop(0, owners, owner, 0)


def partial_body(depths, scaled, hits, ranks, out, table, turned, picks, rows):
    expand_table(ranks, table, turned, picks)
    fetch_rows(depths, table.reshape(-1, LANES), rows)
    owners, _, count = hits.shape
    together = 2

    def several(i, _):
        for k in range(together):
            o = i * together + k
            start = pl.multiple_of(o * count, LANES)
            right = rows[pl.ds(start, count), :].astype(BF16)
            kron = scaled[pl.ds(start, count), :] * jnp.concatenate([right, right], axis=1)
            block = jnp.dot(hits[o], kron, preferred_element_type=F32)
            place = ((o >> 2) & 1) * (owners // 2) + (o >> 3) * 4 + (o & 3)
            out[place] = block.astype(BF16)
        return 0

    lax.fori_loop(0, owners // together, several, 0)


def near_body(near, for_b, for_c):
    for s in range(for_b.shape[0]):
        for_b[s] = near[:, 0]
        for_c[s] = near[:, 1]


def added(copies):
    total = copies[0].astype(F32)
    for s in range(1, copies.shape[0]):
        total = total + copies[s].astype(F32)
    return total


def finish_body(arrived, proj, y, pieces, new_factor):
    total = added(arrived)
    y[...] = total
    gram = lax.dot_general(
        total, total, (((0,), (0,)), ((), ())), precision=lax.Precision.HIGHEST, preferred_element_type=F32
    )
    pieces[...] = gram.astype(BF16).reshape(pieces.shape)
    new_factor[...] = lax.dot_general(
        proj[...], total, (((1,), (1,)), ((), ())), precision=lax.Precision.HIGHEST, preferred_element_type=F32
    )


def cost(flops, nbytes):
    return pl.CostEstimate(flops=flops, transcendentals=0, bytes_accessed=nbytes)


def call(body, out_shape, in_specs, args, scratch=(), limit=16, flops=10**9):
    several = isinstance(out_shape, tuple)
    return pl.pallas_call(
        body,
        out_shape=out_shape,
        in_specs=in_specs,
        out_specs=(VMEM,) * len(out_shape) if several else VMEM,
        scratch_shapes=list(scratch),
        cost_estimate=cost(flops, 10**6),
        compiler_params=pltpu.CompilerParams(vmem_limit_bytes=limit * 2**20),
    )(*args)


def table_scratch(ranks):
    groups = ranks.shape[0] // LANES
    return [
        pltpu.VMEM((groups, PACK, LANES, LANES), F32),
        pltpu.VMEM((groups, LANES, LANES), BF16),
        pltpu.VMEM((PACK // 2, LANES, 2 * LANES), BF16),
    ]


def b_rows(cols, ranks):
    out = jax.ShapeDtypeStruct((cols.shape[0], LANES), F32)
    return call(b_body, out, [SMEM, VMEM], (cols, ranks), table_scratch(ranks))


def scaled_rows(rows, x, target):
    owners, slots, width = target.shape
    out = (
        jax.ShapeDtypeStruct((rows.shape[0], KR), BF16),
        jax.ShapeDtypeStruct((owners, ROWS_DEV, slots * width), BF16),
    )
    return call(scaled_body, out, [VMEM] * 3, (rows, x, target), limit=20)


def partial_blocks(depths, scaled, hits, ranks):
    owners = hits.shape[0]
    out = jax.ShapeDtypeStruct((owners, ROWS_DEV, KR), BF16)
    scratch = [*table_scratch(ranks), pltpu.VMEM((depths.shape[0], LANES), F32)]
    args = (depths, scaled, hits, ranks)
    return call(partial_body, out, [SMEM, VMEM, VMEM, VMEM], args, scratch, limit=32)


def near_copies(near, copies):
    one = jax.ShapeDtypeStruct((copies, near.shape[0], *near.shape[2:]), BF16)
    return call(near_body, (one, one), [VMEM], (near,), flops=10**7)


def finish(arrived, proj, parts):
    out = (
        jax.ShapeDtypeStruct((ROWS_DEV, KR), F32),
        jax.ShapeDtypeStruct((parts, KR // parts, KR), BF16),
        jax.ShapeDtypeStruct((RANK, ROWS_DEV), F32),
    )
    return call(finish_body, out, [VMEM, VMEM], (arrived, proj))


def added_copies(arrived, copies, scale=None):
    def body(arrived, out):
        total = added(arrived)
        total = (total if scale is None else total * scale).astype(BF16)
        for s in range(out.shape[0]):
            out[s] = total

    out = jax.ShapeDtypeStruct((copies, *arrived.shape[1:]), BF16)
    return call(body, out, [VMEM], (arrived,), flops=10**7)


def halves_added(arrived):
    def body(arrived, out):
        for s in range(out.shape[0]):
            out[s] = (arrived[0, s].astype(F32) + arrived[1, s].astype(F32)).astype(BF16)

    out = jax.ShapeDtypeStruct(arrived.shape[1:], BF16)
    return call(body, out, [VMEM], (arrived,), flops=10**7)


def block_moved(index, sizes, order, other):
    block, place = index >> 7, index & (LANES - 1)
    digits = {}
    for name in reversed(order):
        digits[name] = block & (sizes[name] - 1)
        block = block >> (sizes[name].bit_length() - 1)
    moved = 0
    for name in other:
        moved = moved * sizes[name] + digits[name]
    return moved * LANES + place


def update(tile_values, tile_rows, tile_cols, tile_depths, tile_live, factor_b, factor_c, proj):
    n_yh, n_z, n_yl, n_co, n_ka = (lax.axis_size(a) for a in IA_JA_KA)
    owners = n_yl * n_co * n_ka
    tiles, width = tile_values.shape
    slots = tiles // owners
    own = jnp.stack([factor_b[:, 0, :], factor_c[:, 0, :]])
    for_b, for_c = near_copies(to_everyone(own, "z"), n_yh * n_ka)
    ranks_b = exchange(for_b, YH_KA).reshape(-1, LANES)
    near_c = exchange(for_c, Y)
    ranks_c = to_everyone(near_c, "co").reshape(-1, LANES)
    sizes = dict(zip(IA_JA_KA, (n_yh, n_z, n_yl, n_co, n_ka)))
    cols = block_moved(tile_cols, sizes, IA_KA, ("yh", "ka", "z"))
    depths = block_moved(tile_depths, sizes, IA_JA, ("co", "yh", "yl", "z"))
    live = lax.iota(jnp.int32, slots)[None, :] < tile_live.reshape(owners, 1)
    target = jnp.where(live[:, :, None], tile_rows.reshape(owners, slots, width), ROWS_DEV)
    rows = b_rows(cols.reshape(-1), ranks_b)
    scaled, hits = scaled_rows(rows, tile_values.reshape(tiles // PACK, PACK, width), target)
    blocks = partial_blocks(depths.reshape(-1), scaled, hits, ranks_c)
    halves = exchange(blocks, "co").reshape(n_co, owners // n_co, ROWS_DEV, KR)
    arrived = exchange(halves_added(halves), YL_KA)
    y, pieces, new_factor = finish(arrived, proj, n_co * n_ka)
    mine = added_copies(exchange(pieces, CO_KA), n_yh * n_yl)
    mine = added_copies(exchange(mine, Y), n_z)
    mine = added_copies(exchange(mine, "z"), n_co * n_ka, 1.0 / (ROWS_DEV * owners * n_yh * n_z))
    gram = exchange(mine, CO_KA).reshape(KR, KR).astype(F32)
    return y, gram, new_factor


def solution(mesh):
    n_ka = mesh.shape["ka"]
    finer = Mesh(mesh.devices.reshape(2, -1, 4, 2, n_ka), IA_JA_KA)
    in_specs = (
        P(IA_JA_KA, None),
        P(IA_JA_KA, None),
        P(IA_JA_KA, None),
        P(IA_JA_KA, None),
        P(IA_JA_KA, None),
        P(None, JA, IA_KA),
        P(None, "ka", IA_JA),
        P(),
    )
    out_specs = (P(IA_JA_KA, None), P(), P(None, IA_JA_KA))
    return jax.shard_map(update, mesh=finer, in_specs=in_specs, out_specs=out_specs, check_vma=False)
```

time: 151 us -> 160 us (1.060)
  blocking collectives: 74.2 us -> 81.2 us
  local copies, waits for them, and re-layouts: 3.54 us -> 7.17 us
  starting transfers between devices: 24 us -> 20.8 us
  other arithmetic: 1.66 us -> 3.93 us
    all_to_all x7, blocking collectives: 74.2 us -> 81.2 us  [exchange(): return lax.all_to_all(x, axes, split_axis=0, concat_axis=0, tiled=True)]
    unnamed x12 -> x8, local copies, waits for them, and re-layouts: 1.29 us -> 5.44 us
    all_to_all x3, starting transfers between devices: 24 us -> 20.8 us  [exchange(): return lax.all_to_all(x, axes, split_axis=0, concat_axis=0, tiled=True)]
    reshape x2, other arithmetic: 0.05 us -> 1.66 us  [the longest x1 0.83 us: update(): blocks = partial_blocks(depths.reshape(-1), scaled, hits, ranks_c)]
    pallas_call x7 -> x9, Pallas kernels: 29.4 us -> 29.7 us  [call(): pl.pallas_call(body, out_shape=out_shape, in_specs=in_specs, out_specs=(V...]
  transfers between devices with their start and end apart: 3 -> 3, of which waited for: 2 -> 2; matrix products, arithmetic and copies ran while one was open for 0% -> 2% of each run, Pallas kernels for 7% -> 9%
where the time goes in v3:
time: 160 us
  blocking collectives  81.2 us (51%)
  Pallas kernels  29.7 us (19%)
  starting transfers between devices  20.8 us (13%)
  waiting for transfers between devices  16 us (10%)
  local copies, waits for them, and re-layouts  7.17 us (4%)
  other arithmetic  3.93 us (2%)
    all_to_all x7, blocking collectives, exchange(): return lax.all_to_all(x, axes, split_axis=0, concat_axis=0, tiled=True)  81.2 us
    pallas_call x9, Pallas kernels, call(): pl.pallas_call(body, out_shape=out_shape, in_specs=in_specs, out_specs=(V...  29.7 us
    all_to_all x3, starting transfers between devices, exchange(): return lax.all_to_all(x, axes, split_axis=0, concat_axis=0, tiled=True)  20.8 us
    all_to_all x3, waiting for transfers between devices, exchange(): return lax.all_to_all(x, axes, split_axis=0, concat_axis=0, tiled=True)  16 us
    unnamed x8, local copies, waits for them, and re-layouts  5.44 us
  transfers between devices with their start and end apart: 3, of which 2 were waited for; matrix products, arithmetic and copies ran while one was open for 2% of the time, Pallas kernels for 9%

profile of v3, /device:TPU:1, one launch (start us, length us, event | category | flops | bytes accessed | tf_op | source)
XLA Modules:
  0.0 159.5 jit_solution(5990806222383558588)
XLA Ops:
  0.6 0.0 copy-start.2
  0.6 0.7 pad_maximum_fusion
  1.4 17.9 %all_to_all.50.near = bf16[8,2,16,128]{3,2,1,0:T(8,128)(2,1)S(1)} all-to-all(bf16[8,2,16,128]{3,2,1,0:T(8,128)(2,1)S(1)} %broadcast_in_dim.20), channel_id=1, replica_groups=mesh['yh'=2,'z'=8,'yl'=4,'co'=2,'ka'=4] {'z'}, dimensions={0} | all-to-all | bytes 131072 | tf_op jit(solution)/shard_map/all_to_all | solution.py:33
  19.2 0.9 shard_map.103
  20.1 9.3 %all-to-all-start.1 = ((bf16[8,8,16,128]{3,2,1,0:T(8,128)(2,1)}), bf16[8,8,16,128]{3,2,1,0:T(8,128)(2,1)S(1)}, u32[]{:S(2)}, u32[]{:S(2)}) async-start(bf16[8,8,16,128]{3,2,1,0:T(8,128)(2,1)} %get-tuple-element.10), calls=%async_computation.1 | async-start | bytes 524288 | tf_op jit(solution)/shard_map/all_to_all | solution.py:33
  29.4 0.7 iota_compare_fusion
  30.1 0.8 reshape.59
  30.9 0.8 add_bitcast_fusion.cols
  31.8 7.6 %all-to-all-done.1 = bf16[8,8,16,128]{3,2,1,0:T(8,128)(2,1)S(1)} async-done(((bf16[8,8,16,128]{3,2,1,0:T(8,128)(2,1)}), bf16[8,8,16,128]{3,2,1,0:T(8,128)(2,1)S(1)}, u32[]{:S(2)}, u32[]{:S(2)}) %all-to-all-start.1) | async-done | bytes 262176 | tf_op jit(solution)/shard_map/all_to_all | solution.py:33
  39.4 3.4 %all-to-all-start.2 = ((bf16[8,8,16,128]{3,2,1,0:T(8,128)(2,1)}), bf16[8,8,16,128]{3,2,1,0:T(8,128)(2,1)S(1)}, u32[]{:S(2)}, u32[]{:S(2)}) async-start(bf16[8,8,16,128]{3,2,1,0:T(8,128)(2,1)} %get-tuple-element.13), calls=%async_computation.2 | async-start | bytes 524288 | tf_op jit(solution)/shard_map/all_to_all | solution.py:33
  42.8 0.1 broadcast_select_fusion.target
  42.9 0.8 add_bitcast_fusion.1.depths
  43.7 8.4 %all-to-all-done.2 = bf16[8,8,16,128]{3,2,1,0:T(8,128)(2,1)S(1)} async-done(((bf16[8,8,16,128]{3,2,1,0:T(8,128)(2,1)}), bf16[8,8,16,128]{3,2,1,0:T(8,128)(2,1)S(1)}, u32[]{:S(2)}, u32[]{:S(2)}) %all-to-all-start.2) | async-done | bytes 262176 | tf_op jit(solution)/shard_map/all_to_all | solution.py:33
  52.1 0.9 broadcast_in_dim.23
  53.0 8.1 %all-to-all-start.3 = ((bf16[2,8,8,16,128]{4,3,2,1,0:T(8,128)(2,1)}), bf16[2,8,8,16,128]{4,3,2,1,0:T(8,128)(2,1)S(1)}, u32[]{:S(2)}, u32[]{:S(2)}) async-start(bf16[2,8,8,16,128]{4,3,2,1,0:T(8,128)(2,1)} %broadcast_in_dim.23), calls=%async_computation.3 | async-start | bytes 1048576 | tf_op jit(solution)/shard_map/all_to_all | solution.py:33
  61.1 9.2 %shard_map.104.rows = f32[12288,128]{1,0:T(8,128)S(1)} custom-call(s32[12288]{0:T(1024)S(1)} %add_bitcast_fusion.cols, bf16[1024,128]{1,0:T(8,128)(2,1)S(1)} %bitcast.16), custom_call_target="tpu_custom_call" | custom-call | flops 1000000000 | bytes 1000000 | tf_op jit(solution)/shard_map/pallas_call | solution.py:152
  70.3 0.0 copy-done.2
  70.3 5.5 %shard_map.105 = (bf16[12288,256]{1,0:T(8,128)(2,1)S(1)}, bf16[32,64,384]{2,1,0:T(8,128)(2,1)S(1)}) custom-call(f32[12288,128]{1,0:T(8,128)S(1)} %shard_map.104.rows, bf16[12,8,128]{2,1,0:T(8,128)(2,1)S(1)} %bitcast.17, s32[32,3,128]{2,1,0:T(4,128)S(1)} %broadcast_select_fusion.target), custom_call_target="tpu_custom_call" | custom-call | flops 1000000000 | bytes 1000000 | tf_op jit(solution)/shard_map/pallas_call | solution.py:152
  75.8 0.0 copy-start
  75.8 2.6 %copy-done = bf16[12288,256]{1,0:T(8,128)(2,1)} copy-done((bf16[12288,256]{1,0:T(8,128)(2,1)}, bf16[12288,256]{1,0:T(8,128)(2,1)S(1)}, u32[]{:S(2)}) %copy-start) | copy-done | bytes 6291480
  78.5 0.0 all-to-all-done.3
  78.5 0.0 copy-start.1
  78.5 2.8 %copy-done.1 = bf16[12288,256]{1,0:T(8,128)(2,1)S(1)} copy-done((bf16[12288,256]{1,0:T(8,128)(2,1)S(1)}, bf16[12288,256]{1,0:T(8,128)(2,1)}, u32[]{:S(2)}) %copy-start.1) | copy-done | bytes 6291480
  81.3 0.0 copy-start.3
  81.3 12.9 %shard_map.106 = bf16[32,64,256]{2,1,0:T(8,128)(2,1)S(1)} custom-call(s32[12288]{0:T(1024)S(1)} %add_bitcast_fusion.1.depths, bf16[12288,256]{1,0:T(8,128)(2,1)S(1)} %copy-done.1, bf16[32,64,384]{2,1,0:T(8,128)(2,1)S(1)} %get-tuple-element.12.hits, bf16[2048,128]{1,0:T(8,128)(2,1)S(1)} %bitcast.15), custom_call_target="tpu_custom_call" | custom-call | flops 1000000000 | bytes 1000000 | tf_op jit(solution)/shard_map/pallas_call | solution.py:152
  94.2 4.2 %all_to_all.51 = bf16[32,64,256]{2,1,0:T(8,128)(2,1)S(1)} all-to-all(bf16[32,64,256]{2,1,0:T(8,128)(2,1)S(1)} %shard_map.106), channel_id=1, replica_groups=mesh['yh'=2,'z'=8,'yl'=4,'co'=2,'ka'=4] {'co'}, dimensions={0} | all-to-all | bytes 2097152 | tf_op jit(solution)/shard_map/all_to_all | solution.py:33
  98.4 0.1 shard_map.107
  98.5 17.0 %all_to_all.52.arrived = bf16[16,64,256]{2,1,0:T(8,128)(2,1)S(1)} all-to-all(bf16[16,64,256]{2,1,0:T(8,128)(2,1)S(1)} %shard_map.107), channel_id=1, replica_groups=mesh['yh'=2,'z'=8,'yl'=4,'co'=2,'ka'=4] {'yl','ka'}, dimensions={0} | all-to-all | bytes 1048576 | tf_op jit(solution)/shard_map/all_to_all | solution.py:33
  115.5 0.0 copy-done.3
  115.5 1.1 shard_map.108
  116.6 10.1 %all_to_all.53.arrived = bf16[8,32,256]{2,1,0:T(8,128)(2,1)S(1)} all-to-all(bf16[8,32,256]{2,1,0:T(8,128)(2,1)S(1)} %get-tuple-element.15), channel_id=1, replica_groups=mesh['yh'=2,'z'=8,'yl'=4,'co'=2,'ka'=4] {'co','ka'}, dimensions={0} | all-to-all | bytes 262144 | tf_op jit(solution)/shard_map/all_to_all | solution.py:33
  126.7 10.4 %all_to_all.54.arrived = bf16[8,32,256]{2,1,0:T(8,128)(2,1)S(1)} all-to-all(bf16[8,32,256]{2,1,0:T(8,128)(2,1)S(1)} %shard_map.109), channel_id=1, replica_groups=mesh['yh'=2,'z'=8,'yl'=4,'co'=2,'ka'=4] {'yh','yl'}, dimensions={0} | all-to-all | bytes 262144 | tf_op jit(solution)/shard_map/all_to_all | solution.py:33
  137.2 10.4 %all_to_all.55.arrived = bf16[8,32,256]{2,1,0:T(8,128)(2,1)S(1)} all-to-all(bf16[8,32,256]{2,1,0:T(8,128)(2,1)S(1)} %shard_map.110), channel_id=1, replica_groups=mesh['yh'=2,'z'=8,'yl'=4,'co'=2,'ka'=4] {'z'}, dimensions={0} | all-to-all | bytes 262144 | tf_op jit(solution)/shard_map/all_to_all | solution.py:33
  147.6 11.2 %all_to_all.56 = bf16[8,32,256]{2,1,0:T(8,128)(2,1)S(1)} all-to-all(bf16[8,32,256]{2,1,0:T(8,128)(2,1)S(1)} %shard_map.111), channel_id=1, replica_groups=mesh['yh'=2,'z'=8,'yl'=4,'co'=2,'ka'=4] {'co','ka'}, dimensions={0} | all-to-all | bytes 262144 | tf_op jit(solution)/shard_map/all_to_all | solution.py:33
  158.8 0.7 bitcast_convert_fusion
  (4 shorter events, 0.1 us)
Async XLA Ops:
  0.6 69.7 %copy-start.2 = (bf16[96,128]{1,0:T(8,128)(2,1)S(1)}, bf16[96,128]{1,0:T(8,128)(2,1)}, u32[]{:S(2)}) copy-start(bf16[96,128]{1,0:T(8,128)(2,1)} %param.8) | copy-start | bytes 73732
  20.1 19.3 %all-to-all-start.1 = ((bf16[8,8,16,128]{3,2,1,0:T(8,128)(2,1)}), bf16[8,8,16,128]{3,2,1,0:T(8,128)(2,1)S(1)}, u32[]{:S(2)}, u32[]{:S(2)}) async-start(bf16[8,8,16,128]{3,2,1,0:T(8,128)(2,1)} %get-tuple-element.10), calls=%async_computation.1 | async-start | bytes 524288 | tf_op jit(solution)/shard_map/all_to_all | solution.py:33
  39.4 12.8 %all-to-all-start.2 = ((bf16[8,8,16,128]{3,2,1,0:T(8,128)(2,1)}), bf16[8,8,16,128]{3,2,1,0:T(8,128)(2,1)S(1)}, u32[]{:S(2)}, u32[]{:S(2)}) async-start(bf16[8,8,16,128]{3,2,1,0:T(8,128)(2,1)} %get-tuple-element.13), calls=%async_computation.2 | async-start | bytes 524288 | tf_op jit(solution)/shard_map/all_to_all | solution.py:33
  53.0 25.4 %all-to-all-start.3 = ((bf16[2,8,8,16,128]{4,3,2,1,0:T(8,128)(2,1)}), bf16[2,8,8,16,128]{4,3,2,1,0:T(8,128)(2,1)S(1)}, u32[]{:S(2)}, u32[]{:S(2)}) async-start(bf16[2,8,8,16,128]{4,3,2,1,0:T(8,128)(2,1)} %broadcast_in_dim.23), calls=%async_computation.3 | async-start | bytes 1048576 | tf_op jit(solution)/shard_map/all_to_all | solution.py:33
  75.8 2.7 %copy-start = (bf16[12288,256]{1,0:T(8,128)(2,1)}, bf16[12288,256]{1,0:T(8,128)(2,1)S(1)}, u32[]{:S(2)}) copy-start(bf16[12288,256]{1,0:T(8,128)(2,1)S(1)} %get-tuple-element.11.scaled) | copy-start | bytes 18874372
  78.5 2.8 %copy-start.1 = (bf16[12288,256]{1,0:T(8,128)(2,1)S(1)}, bf16[12288,256]{1,0:T(8,128)(2,1)}, u32[]{:S(2)}) copy-start(bf16[12288,256]{1,0:T(8,128)(2,1)} %copy-done) | copy-start | bytes 18874372
  81.3 34.3 %copy-start.3 = (f32[16,256]{1,0:T(8,128)S(1)}, f32[16,256]{1,0:T(8,128)}, u32[]{:S(2)}) copy-start(f32[16,256]{1,0:T(8,128)} %proj.1) | copy-start | bytes 49156

commit v4 on v3

v4 whole, which is shorter than its diff:
```python
import jax
import jax.numpy as jnp
from jax import lax
from jax.experimental import pallas as pl
from jax.experimental.pallas import tpu as pltpu
from jax.sharding import Mesh
from jax.sharding import PartitionSpec as P

RANK = 16
KR = RANK * RANK
ROWS_DEV = 64
LANES = 128
PACK = LANES // RANK
JA = ("yl", "co")
IA_KA = ("ia", "ka")
IA_YL = ("ia", "yl")
IA_JA = ("ia", "yl", "co")
CO_KA = ("co", "ka")
YL_KA = ("yl", "ka")
IA_JA_KA = ("ia", "yl", "co", "ka")
BF16 = jnp.bfloat16
F32 = jnp.float32
VMEM = pl.BlockSpec(memory_space=pltpu.VMEM)
SMEM = pl.BlockSpec(memory_space=pltpu.SMEM)
HBM = pl.BlockSpec(memory_space=pltpu.HBM)


def iota(shape, dim):
    return lax.broadcasted_iota(jnp.int32, shape, dim)


def exchange(x, axes):
    return lax.all_to_all(x, axes, split_axis=0, concat_axis=0, tiled=True)


def to_everyone(x, axes):
    return exchange(jnp.broadcast_to(x, (lax.axis_size(axes), *x.shape)), axes)


def turn(ranks, turned, first=0):
    for g in range(ranks.shape[0] // LANES):
        turned[first + g] = ranks[g * LANES : (g + 1) * LANES, :].T


def fetch_rows(views, table, rows, start, count, high):
    for r in range(count):
        rows[pl.ds(r * high, high), :] = table[pl.ds(views[r][start], high), :]


def views_of(index, count):
    return [index.at[pl.ds(r, index.shape[0] - r)] for r in range(count)]


def scaled_body(cols, x, ranks, out, table, turned, picks, rows, scaled, done):
    turn(ranks, turned)
    groups = turned.shape[0]
    row, lane = iota((LANES, KR), 0), iota((LANES, KR), 1)
    for j in range(PACK):
        picks[j] = (((row >> 4) == j) & ((row & 15) == (lane >> 4))).astype(BF16)

    def pick(j, _):
        for g in range(groups):
            both = jnp.dot(turned[g], picks[j], preferred_element_type=F32)
            start = pl.multiple_of((g * PACK + j) * 2 * LANES, 2 * LANES)
            table[pl.ds(start, LANES, 2), :] = both[:, :LANES]
            table[pl.ds(start + 1, LANES, 2), :] = both[:, LANES:]
        return 0

    lax.fori_loop(0, PACK, pick, 0)
    tiles = x.shape[1]
    count = tiles * LANES
    views = views_of(cols, count)

    def sent(g):
        part = pl.ds(pl.multiple_of(g * count, count), count)
        return pltpu.make_async_copy(scaled.at[part], out.at[part], done.at[g])

    def group(g, _):
        fetch_rows(views, table, rows, g * count, count, 2)
        xs = x[g].astype(F32).T
        for j in range(tiles):
            by = xs[:, j : j + 1]
            left = rows[pl.ds(j * 2 * LANES, LANES, 2), :] * by
            right = rows[pl.ds(j * 2 * LANES + 1, LANES, 2), :] * by
            start = pl.multiple_of(g * count + j * LANES, LANES)
            scaled[pl.ds(start, LANES), :] = jnp.concatenate([left, right], axis=1).astype(BF16)
        sent(g).start()
        return 0

    lax.fori_loop(0, x.shape[0], group, 0)

    def wait(g, _):
        sent(g).wait()
        return 0

    lax.fori_loop(0, x.shape[0], wait, 0)


def partial_body(depths, scaled, target, ranks, ranks_other, out, table, turned, picks, rows, index, left, done):
    indices = pltpu.make_async_copy(depths, index, done.at[0])
    lefts = pltpu.make_async_copy(scaled, left, done.at[1])
    indices.start()
    lefts.start()
    turn(ranks, turned)
    turn(ranks_other, turned, turned.shape[0] // 2)
    groups = turned.shape[0]
    row, lane = iota((LANES, 2 * LANES), 0), iota((LANES, 2 * LANES), 1)
    for j in range(PACK // 2):
        picks[j] = (((row >> 4) == 2 * j + (lane >> 7)) & ((row & 15) == (lane & 15))).astype(BF16)

    def pick(j, _):
        for g in range(groups):
            two = jnp.dot(turned[g], picks[j], preferred_element_type=F32)
            start = pl.multiple_of((g * PACK + 2 * j) * LANES, 2 * LANES)
            table[pl.ds(start, LANES), :] = two[:, :LANES]
            table[pl.ds(start + LANES, LANES), :] = two[:, LANES:]
        return 0

    lax.fori_loop(0, PACK // 2, pick, 0)
    indices.wait()
    step = 8 * LANES
    views = views_of(index, step)

    def several_rows(g, _):
        start = pl.multiple_of(g * step, step)
        fetch_rows(views, table, rows.at[pl.ds(start, step)], start, step, 1)
        return 0

    lax.fori_loop(0, rows.shape[0] // step, several_rows, 0)
    lefts.wait()
    owners, slots, _ = target.shape
    count = slots * LANES
    together = 2

    def several(i, _):
        for k in range(together):
            o = i * together + k
            start = pl.multiple_of(o * count, LANES)
            right = rows[pl.ds(start, count), :].astype(BF16)
            kron = left[pl.ds(start, count), :] * jnp.concatenate([right, right], axis=1)
            owner_rows = target[o]
            hits = [(iota((ROWS_DEV, LANES), 0) == owner_rows[t : t + 1, :]).astype(BF16) for t in range(slots)]
            block = jnp.dot(jnp.concatenate(hits, axis=1), kron, preferred_element_type=F32)
            place = ((o >> 2) & 1) * (owners // 2) + (o >> 3) * 4 + (o & 3)
            out[place] = block.astype(BF16)
        return 0

    lax.fori_loop(0, owners // together, several, 0)


def added(copies):
    total = copies[0].astype(F32)
    for s in range(1, copies.shape[0]):
        total = total + copies[s].astype(F32)
    return total


def finish_body(arrived, proj, y, pieces, new_factor):
    total = added(arrived)
    y[...] = total
    gram = lax.dot_general(
        total, total, (((0,), (0,)), ((), ())), precision=lax.Precision.HIGHEST, preferred_element_type=F32
    )
    pieces[...] = gram.astype(BF16).reshape(pieces.shape)
    new_factor[...] = lax.dot_general(
        proj[...], total, (((1,), (1,)), ((), ())), precision=lax.Precision.HIGHEST, preferred_element_type=F32
    )


def cost(flops, nbytes):
    return pl.CostEstimate(flops=flops, transcendentals=0, bytes_accessed=nbytes)


def call(body, out_shape, in_specs, args, scratch=(), limit=16, flops=10**9, out_spec=VMEM):
    several = isinstance(out_shape, tuple)
    return pl.pallas_call(
        body,
        out_shape=out_shape,
        in_specs=in_specs,
        out_specs=(out_spec,) * len(out_shape) if several else out_spec,
        scratch_shapes=list(scratch),
        cost_estimate=cost(flops, 10**6),
        compiler_params=pltpu.CompilerParams(vmem_limit_bytes=limit * 2**20),
    )(*args)


def scaled_rows(cols, x, ranks):
    groups, tiles, _ = x.shape
    out = pltpu.HBM((cols.shape[0], KR), BF16)
    scratch = [
        pltpu.VMEM((ranks.shape[0] * PACK * 2, LANES), F32),
        pltpu.VMEM((ranks.shape[0] // LANES, LANES, LANES), BF16),
        pltpu.VMEM((PACK, LANES, KR), BF16),
        pltpu.VMEM((tiles * LANES * 2, LANES), F32),
        pltpu.VMEM(out.shape, BF16),
        pltpu.SemaphoreType.DMA((groups,)),
    ]
    return call(scaled_body, out, [SMEM, VMEM, VMEM], (cols, x, ranks), scratch, limit=24, out_spec=HBM)


def partial_blocks(depths, scaled, target, ranks, ranks_other):
    owners = target.shape[0]
    groups = 2 * ranks.shape[0] // LANES
    out = jax.ShapeDtypeStruct((owners, ROWS_DEV, KR), BF16)
    scratch = [
        pltpu.VMEM((groups * PACK * LANES, LANES), F32),
        pltpu.VMEM((groups, LANES, LANES), BF16),
        pltpu.VMEM((PACK // 2, LANES, 2 * LANES), BF16),
        pltpu.VMEM((depths.shape[0], LANES), F32),
        pltpu.SMEM(depths.shape, jnp.int32),
        pltpu.VMEM(scaled.shape, BF16),
        pltpu.SemaphoreType.DMA((2,)),
    ]
    scaled = pltpu.with_memory_space_constraint(scaled, pltpu.HBM)
    args = (depths, scaled, target, ranks, ranks_other)
    return call(partial_body, out, [HBM, HBM, VMEM, VMEM, VMEM], args, scratch, limit=32)


def finish(arrived, proj, parts):
    out = (
        jax.ShapeDtypeStruct((ROWS_DEV, KR), F32),
        jax.ShapeDtypeStruct((parts, KR // parts, KR), BF16),
        jax.ShapeDtypeStruct((RANK, ROWS_DEV), F32),
    )
    return call(finish_body, out, [VMEM, VMEM], (arrived, proj))


def added_copies(arrived, copies, scale=None):
    def body(arrived, out):
        total = added(arrived)
        total = (total if scale is None else total * scale).astype(BF16)
        for s in range(out.shape[0]):
            out[s] = total

    out = jax.ShapeDtypeStruct((copies, *arrived.shape[1:]), BF16)
    return call(body, out, [VMEM], (arrived,), flops=10**7)


def halves_added(arrived):
    def body(arrived, out):
        for s in range(out.shape[0]):
            out[s] = (arrived[0, s].astype(F32) + arrived[1, s].astype(F32)).astype(BF16)

    out = jax.ShapeDtypeStruct(arrived.shape[1:], BF16)
    return call(body, out, [VMEM], (arrived,), flops=10**7)


def update(tile_values, tile_rows, tile_cols, tile_depths, tile_live, factor_b, factor_c, proj):
    n_ia, n_yl, n_co, n_ka = (lax.axis_size(a) for a in IA_JA_KA)
    owners = n_yl * n_co * n_ka
    tiles, width = tile_values.shape
    slots = tiles // owners
    ranks_b = to_everyone(factor_b[:, 0, :], IA_KA).reshape(-1, LANES)
    ranks_c = to_everyone(factor_c[:, 0, :], IA_YL).reshape(-1, LANES)
    ranks_other = lax.ppermute(ranks_c, "co", [(0, 1), (1, 0)])
    block = tile_depths >> 7
    half = (block ^ lax.axis_index("co")) & 1
    depths = (half * (n_ia * n_yl) + (block >> 1)) * LANES + (tile_depths & (LANES - 1))
    cols = tile_cols * 2
    live = lax.iota(jnp.int32, slots)[None, :] < tile_live.reshape(owners, 1)
    target = jnp.where(live[:, :, None], tile_rows.reshape(owners, slots, width), ROWS_DEV)
    scaled = scaled_rows(cols.reshape(-1), tile_values.reshape(tiles // PACK, PACK, width), ranks_b)
    blocks = partial_blocks(depths.reshape(-1), scaled, target, ranks_c, ranks_other)
    halves = exchange(blocks, "co").reshape(n_co, owners // n_co, ROWS_DEV, KR)
    arrived = exchange(halves_added(halves), YL_KA)
    y, pieces, new_factor = finish(arrived, proj, n_co * n_ka)
    mine = added_copies(exchange(pieces, CO_KA), n_yl)
    mine = added_copies(exchange(mine, "yl"), n_ia)
    mine = added_copies(exchange(mine, "ia"), n_co * n_ka, 1.0 / (ROWS_DEV * owners * n_ia))
    gram = exchange(mine, CO_KA).reshape(KR, KR).astype(F32)
    return y, gram, new_factor


def solution(mesh):
    n_ka = mesh.shape["ka"]
    finer = Mesh(mesh.devices.reshape(-1, 4, 2, n_ka), IA_JA_KA)
    in_specs = (
        P(IA_JA_KA, None),
        P(IA_JA_KA, None),
        P(IA_JA_KA, None),
        P(IA_JA_KA, None),
        P(IA_JA_KA, None),
        P(None, JA, IA_KA),
        P(None, "ka", IA_JA),
        P(),
    )
    out_specs = (P(IA_JA_KA, None), P(), P(None, IA_JA_KA))
    return jax.shard_map(update, mesh=finer, in_specs=in_specs, out_specs=out_specs, check_vma=False)
```

time: 160 us -> 154 us (0.963)
  blocking collectives: 81.2 us -> 69.8 us
  starting transfers between devices: 20.8 us -> 28.2 us
  waiting for transfers between devices: 16 us -> 20.8 us
  Pallas kernels: 29.7 us -> 26.2 us
  local copies, waits for them, and re-layouts: 7.17 us -> 4.41 us
    all_to_all x7 -> x6, blocking collectives: 81.2 us -> 69.8 us  [exchange(): return lax.all_to_all(x, axes, split_axis=0, concat_axis=0, tiled=True)]
    all_to_all x3 -> x2, waiting for transfers between devices: 16 us -> 20.8 us  [exchange(): return lax.all_to_all(x, axes, split_axis=0, concat_axis=0, tiled=True)]
    unnamed x8 -> x4, local copies, waits for them, and re-layouts: 5.44 us -> 0.74 us
    all_to_all x3 -> x2, starting transfers between devices: 20.8 us -> 25.3 us  [exchange(): return lax.all_to_all(x, axes, split_axis=0, concat_axis=0, tiled=True)]
    pallas_call x9 -> x7, Pallas kernels: 29.7 us -> 26.2 us  [call(): pl.pallas_call(body, out_shape=out_shape, in_specs=in_specs, out_specs=(o...]
    ppermute x0 -> x1, starting transfers between devices: none -> 2.94 us  [update(): ranks_other = lax.ppermute(ranks_c, 'co', [(0, 1), (1, 0)])]
    broadcast_in_dim x2, local copies, waits for them, and re-layouts: 0.92 us -> 2.85 us  [to_everyone(): return exchange(jnp.broadcast_to(x, (lax.axis_size(axes), *x.shape)), axes)]
where the time goes in v4:
time: 154 us; the launch traced here: 153 us
  blocking collectives  69.8 us (45%)
  starting transfers between devices  28.2 us (18%)
  Pallas kernels  26.2 us (17%)
  waiting for transfers between devices  20.8 us (14%)
  local copies, waits for them, and re-layouts  4.41 us (3%)
  other arithmetic  3.19 us (2%)
    all_to_all x6, blocking collectives, exchange(): return lax.all_to_all(x, axes, split_axis=0, concat_axis=0, tiled=True)  69.8 us
    pallas_call x7, Pallas kernels, call(): pl.pallas_call(body, out_shape=out_shape, in_specs=in_specs, out_specs=(o...  26.2 us
    all_to_all x2, starting transfers between devices, exchange(): return lax.all_to_all(x, axes, split_axis=0, concat_axis=0, tiled=True)  25.3 us
    all_to_all x2, waiting for transfers between devices, exchange(): return lax.all_to_all(x, axes, split_axis=0, concat_axis=0, tiled=True)  20.8 us
  transfers between devices with their start and end apart: 3, of which 2 were waited for; matrix products, arithmetic and copies ran while one was open for 2% of the time, Pallas kernels for 9%

profile of v4, /device:TPU:1, one launch (start us, length us, event | category | flops | bytes accessed | tf_op | source)
XLA Modules:
  0.0 153.4 jit_solution(770559970610808579)
XLA Ops:
  0.6 1.4 broadcast_in_dim.23
  2.1 17.1 %all-to-all-start.1 = ((bf16[64,16,128]{2,1,0:T(8,128)(2,1)}), bf16[64,16,128]{2,1,0:T(8,128)(2,1)S(1)}, u32[]{:S(2)}, u32[]{:S(2)}) async-start(bf16[64,16,128]{2,1,0:T(8,128)(2,1)} %broadcast_in_dim.23), calls=%async_computation.1 | async-start | bytes 524288 | tf_op jit(solution)/shard_map/all_to_all | solution.py:33
  19.2 0.8 multiply_bitcast_fusion.cols
  20.0 12.3 %all-to-all-done.1 = bf16[64,16,128]{2,1,0:T(8,128)(2,1)S(1)} async-done(((bf16[64,16,128]{2,1,0:T(8,128)(2,1)}), bf16[64,16,128]{2,1,0:T(8,128)(2,1)S(1)}, u32[]{:S(2)}, u32[]{:S(2)}) %all-to-all-start.1) | async-done | bytes 262176 | tf_op jit(solution)/shard_map/all_to_all | solution.py:33
  32.3 1.4 broadcast_in_dim.20
  33.7 8.1 %all-to-all-start = ((bf16[64,16,128]{2,1,0:T(8,128)(2,1)}), bf16[64,16,128]{2,1,0:T(8,128)(2,1)S(1)}, u32[]{:S(2)}, u32[]{:S(2)}) async-start(bf16[64,16,128]{2,1,0:T(8,128)(2,1)} %broadcast_in_dim.20), calls=%async_computation | async-start | bytes 524288 | tf_op jit(solution)/shard_map/all_to_all | solution.py:33
  41.9 0.8 add_bitcast_fusion.depths
  42.7 0.8 reshape.59
  43.5 0.7 iota_compare_fusion
  44.3 2.9 %collective-permute-start = (bf16[1024,128]{1,0:T(8,128)(2,1)S(1)}, bf16[1024,128]{1,0:T(8,128)(2,1)S(1)}, u32[]{:S(2)}, u32[]{:S(2)}) collective-permute-start(bf16[1024,128]{1,0:T(8,128)(2,1)S(1)} %bitcast.15), channel_id=1, source_target_pairs={{0,4},{4,0},{1,5},{5,1},{2,6},{6,2},{3,7},{7,3},{8,12},{12,8},{9,1... | collective-permute-start | bytes 786440 | tf_op jit(solution)/shard_map/ppermute | solution.py:255
  47.2 0.1 broadcast_select_fusion.target
  47.3 8.5 %all-to-all-done = bf16[64,16,128]{2,1,0:T(8,128)(2,1)S(1)} async-done(((bf16[64,16,128]{2,1,0:T(8,128)(2,1)}), bf16[64,16,128]{2,1,0:T(8,128)(2,1)S(1)}, u32[]{:S(2)}, u32[]{:S(2)}) %all-to-all-start) | async-done | bytes 262176 | tf_op jit(solution)/shard_map/all_to_all | solution.py:33
  55.8 0.0 copy-start
  55.8 0.7 copy-done
  56.6 13.3 %shard_map.103.scaled = bf16[12288,256]{1,0:T(8,128)(2,1)} custom-call(s32[12288]{0:T(1024)S(1)} %multiply_bitcast_fusion.cols, bf16[12,8,128]{2,1,0:T(8,128)(2,1)S(1)} %bitcast.18, bf16[1024,128]{1,0:T(8,128)(2,1)S(1)} %bitcast.17), custom_call_target="tpu_custom_call" | custom-call | flops 1000000000 | bytes 1000000 | tf_op jit(solution)/shard_map/pallas_call | solution.py:176
  69.9 0.0 copy-start.1
  69.9 0.0 collective-permute-done.ranks_other
  69.9 11.6 %shard_map.104 = bf16[32,64,256]{2,1,0:T(8,128)(2,1)S(1)} custom-call(s32[12288]{0:T(1024)S(1)} %add_bitcast_fusion.depths, bf16[12288,256]{1,0:T(8,128)(2,1)} %shard_map.103.scaled, s32[32,3,128]{2,1,0:T(4,128)S(1)} %broadcast_select_fusion.target, bf16[1024,128]{1,0:T(8,128)(2,1)S(1)} %bitcast.16, bf16[1024,128]{1,0:T(8,128)(2,1)S(1)} %collective-permute-done.ranks_other), custom_call_target="tpu_custom_call" | custom-call | flops 1000000000 | bytes 1000000 | tf_op jit(solution)/shard_map/pallas_call | solution.py:176
  81.5 7.6 %all_to_all.40 = bf16[32,64,256]{2,1,0:T(8,128)(2,1)S(1)} all-to-all(bf16[32,64,256]{2,1,0:T(8,128)(2,1)S(1)} %shard_map.104), channel_id=1, replica_groups=mesh['ia'=16,'yl'=4,'co'=2,'ka'=4] {'co'}, dimensions={0} | all-to-all | bytes 2097152 | tf_op jit(solution)/shard_map/all_to_all | solution.py:33
  89.1 0.1 shard_map.105
  89.2 19.7 %all_to_all.41.arrived = bf16[16,64,256]{2,1,0:T(8,128)(2,1)S(1)} all-to-all(bf16[16,64,256]{2,1,0:T(8,128)(2,1)S(1)} %shard_map.105), channel_id=1, replica_groups=mesh['ia'=16,'yl'=4,'co'=2,'ka'=4] {'yl','ka'}, dimensions={0} | all-to-all | bytes 1048576 | tf_op jit(solution)/shard_map/all_to_all | solution.py:33
  108.9 0.0 copy-done.1
  108.9 1.1 shard_map.106
  110.0 10.3 %all_to_all.42.arrived = bf16[8,32,256]{2,1,0:T(8,128)(2,1)S(1)} all-to-all(bf16[8,32,256]{2,1,0:T(8,128)(2,1)S(1)} %get-tuple-element.7), channel_id=1, replica_groups=mesh['ia'=16,'yl'=4,'co'=2,'ka'=4] {'co','ka'}, dimensions={0} | all-to-all | bytes 262144 | tf_op jit(solution)/shard_map/all_to_all | solution.py:33
  120.4 7.2 %all_to_all.43.arrived = bf16[4,32,256]{2,1,0:T(8,128)(2,1)S(1)} all-to-all(bf16[4,32,256]{2,1,0:T(8,128)(2,1)S(1)} %shard_map.107), channel_id=1, replica_groups=mesh['ia'=16,'yl'=4,'co'=2,'ka'=4] {'yl'}, dimensions={0} | all-to-all | bytes 131072 | tf_op jit(solution)/shard_map/all_to_all | solution.py:33
  127.6 14.1 %all_to_all.44.arrived = bf16[16,32,256]{2,1,0:T(8,128)(2,1)S(1)} all-to-all(bf16[16,32,256]{2,1,0:T(8,128)(2,1)S(1)} %shard_map.108), channel_id=1, replica_groups=mesh['ia'=16,'yl'=4,'co'=2,'ka'=4] {'ia'}, dimensions={0} | all-to-all | bytes 524288 | tf_op jit(solution)/shard_map/all_to_all | solution.py:33
  141.7 10.9 %all_to_all.45 = bf16[8,32,256]{2,1,0:T(8,128)(2,1)S(1)} all-to-all(bf16[8,32,256]{2,1,0:T(8,128)(2,1)S(1)} %shard_map.109), channel_id=1, replica_groups=mesh['ia'=16,'yl'=4,'co'=2,'ka'=4] {'co','ka'}, dimensions={0} | all-to-all | bytes 262144 | tf_op jit(solution)/shard_map/all_to_all | solution.py:33
  152.7 0.7 bitcast_convert_fusion
  (3 shorter events, 0.1 us)
Async XLA Ops:
  2.1 30.2 %all-to-all-start.1 = ((bf16[64,16,128]{2,1,0:T(8,128)(2,1)}), bf16[64,16,128]{2,1,0:T(8,128)(2,1)S(1)}, u32[]{:S(2)}, u32[]{:S(2)}) async-start(bf16[64,16,128]{2,1,0:T(8,128)(2,1)} %broadcast_in_dim.23), calls=%async_computation.1 | async-start | bytes 524288 | tf_op jit(solution)/shard_map/all_to_all | solution.py:33
  33.7 22.1 %all-to-all-start = ((bf16[64,16,128]{2,1,0:T(8,128)(2,1)}), bf16[64,16,128]{2,1,0:T(8,128)(2,1)S(1)}, u32[]{:S(2)}, u32[]{:S(2)}) async-start(bf16[64,16,128]{2,1,0:T(8,128)(2,1)} %broadcast_in_dim.20), calls=%async_computation | async-start | bytes 524288 | tf_op jit(solution)/shard_map/all_to_all | solution.py:33
  44.3 25.6 %collective-permute-start = (bf16[1024,128]{1,0:T(8,128)(2,1)S(1)}, bf16[1024,128]{1,0:T(8,128)(2,1)S(1)}, u32[]{:S(2)}, u32[]{:S(2)}) collective-permute-start(bf16[1024,128]{1,0:T(8,128)(2,1)S(1)} %bitcast.15), channel_id=1, source_target_pairs={{0,4},{4,0},{1,5},{5,1},{2,6},{6,2},{3,7},{7,3},{8,12},{12,8},{9,1... | collective-permute-start | bytes 786440 | tf_op jit(solution)/shard_map/ppermute | solution.py:255
  55.8 0.7 copy-start
  69.9 39.1 %copy-start.1 = (f32[16,256]{1,0:T(8,128)S(1)}, f32[16,256]{1,0:T(8,128)}, u32[]{:S(2)}) copy-start(f32[16,256]{1,0:T(8,128)} %proj.1) | copy-start | bytes 49156

commit v5 on v4

--- a/solution.py
+++ b/solution.py
@@ -51,7 +51,11 @@
     return [index.at[pl.ds(r, index.shape[0] - r)] for r in range(count)]
 
 
-def scaled_body(cols, x, ranks, out, table, turned, picks, rows, scaled, done):
+def scaled_body(cols, x, ranks, out, table, turned, picks, rows, scaled, index, values, done, ready):
+    indices = pltpu.make_async_copy(cols, index, ready.at[0])
+    values_in = pltpu.make_async_copy(x, values, ready.at[1])
+    indices.start()
+    values_in.start()
     turn(ranks, turned)
     groups = turned.shape[0]
     row, lane = iota((LANES, KR), 0), iota((LANES, KR), 1)
@@ -67,9 +71,11 @@
         return 0
 
     lax.fori_loop(0, PACK, pick, 0)
+    indices.wait()
+    values_in.wait()
     tiles = x.shape[1]
     count = tiles * LANES
-    views = views_of(cols, count)
+    views = views_of(index, count)
 
     def sent(g):
         part = pl.ds(pl.multiple_of(g * count, count), count)
@@ -77,7 +83,7 @@
 
     def group(g, _):
         fetch_rows(views, table, rows, g * count, count, 2)
-        xs = x[g].astype(F32).T
+        xs = values[g].astype(F32).T
         for j in range(tiles):
             by = xs[:, j : j + 1]
             left = rows[pl.ds(j * 2 * LANES, LANES, 2), :] * by
@@ -186,6 +192,7 @@
 
 def scaled_rows(cols, x, ranks):
     groups, tiles, _ = x.shape
+    x = pltpu.with_memory_space_constraint(x, pltpu.HBM)
     out = pltpu.HBM((cols.shape[0], KR), BF16)
     scratch = [
         pltpu.VMEM((ranks.shape[0] * PACK * 2, LANES), F32),
@@ -193,9 +200,12 @@
         pltpu.VMEM((PACK, LANES, KR), BF16),
         pltpu.VMEM((tiles * LANES * 2, LANES), F32),
         pltpu.VMEM(out.shape, BF16),
+        pltpu.SMEM(cols.shape, jnp.int32),
+        pltpu.VMEM(x.shape, BF16),
         pltpu.SemaphoreType.DMA((groups,)),
+        pltpu.SemaphoreType.DMA((2,)),
     ]
-    return call(scaled_body, out, [SMEM, VMEM, VMEM], (cols, x, ranks), scratch, limit=24, out_spec=HBM)
+    return call(scaled_body, out, [HBM, HBM, VMEM], (cols, x, ranks), scratch, limit=24, out_spec=HBM)
 
 
 def partial_blocks(depths, scaled, target, ranks, ranks_other):
@@ -251,16 +261,17 @@
     tiles, width = tile_values.shape
     slots = tiles // owners
     ranks_b = to_everyone(factor_b[:, 0, :], IA_KA).reshape(-1, LANES)
-    ranks_c = to_everyone(factor_c[:, 0, :], IA_YL).reshape(-1, LANES)
+    for_c = jnp.broadcast_to(factor_c[:, 0, :], (n_ia * n_yl, RANK, LANES))
+    ranks_c = exchange(for_c, IA_YL).reshape(-1, LANES)
     ranks_other = lax.ppermute(ranks_c, "co", [(0, 1), (1, 0)])
     block = tile_depths >> 7
     half = (block ^ lax.axis_index("co")) & 1
-    depths = (half * (n_ia * n_yl) + (block >> 1)) * LANES + (tile_depths & (LANES - 1))
-    cols = tile_cols * 2
+    depths = ((half * (n_ia * n_yl) + (block >> 1)) * LANES + (tile_depths & (LANES - 1))).reshape(-1)
+    cols = (tile_cols * 2).reshape(-1)
     live = lax.iota(jnp.int32, slots)[None, :] < tile_live.reshape(owners, 1)
     target = jnp.where(live[:, :, None], tile_rows.reshape(owners, slots, width), ROWS_DEV)
-    scaled = scaled_rows(cols.reshape(-1), tile_values.reshape(tiles // PACK, PACK, width), ranks_b)
-    blocks = partial_blocks(depths.reshape(-1), scaled, target, ranks_c, ranks_other)
+    scaled = scaled_rows(cols, tile_values.reshape(tiles // PACK, PACK, width), ranks_b)
+    blocks = partial_blocks(depths, scaled, target, ranks_c, ranks_other)
     halves = exchange(blocks, "co").reshape(n_co, owners // n_co, ROWS_DEV, KR)
     arrived = exchange(halves_added(halves), YL_KA)
     y, pieces, new_factor = finish(arrived, proj, n_co * n_ka)

time: 154 us -> 152 us (0.987)
  transfers between devices with their start and end apart: 3 -> 3, of which waited for: 2 -> 2; matrix products, arithmetic and copies ran while one was open for 2% -> 2% of each run, Pallas kernels for 9% -> 8%
where the time goes in v5:
time: 152 us; the launch traced here: 151 us
  blocking collectives  69.8 us (46%)
  starting transfers between devices  28.2 us (19%)
  Pallas kernels  25 us (16%)
  waiting for transfers between devices  20.8 us (14%)
  local copies, waits for them, and re-layouts  3.68 us (2%)
  other arithmetic  3.19 us (2%)
    all_to_all x6, blocking collectives, exchange(): return lax.all_to_all(x, axes, split_axis=0, concat_axis=0, tiled=True)  69.8 us
    all_to_all x2, starting transfers between devices, exchange(): return lax.all_to_all(x, axes, split_axis=0, concat_axis=0, tiled=True)  25.3 us
    pallas_call x7, Pallas kernels, call(): pl.pallas_call(body, out_shape=out_shape, in_specs=in_specs, out_specs=(o...  25 us
    all_to_all x2, waiting for transfers between devices, exchange(): return lax.all_to_all(x, axes, split_axis=0, concat_axis=0, tiled=True)  20.8 us
  transfers between devices with their start and end apart: 3, of which 2 were waited for; matrix products, arithmetic and copies ran while one was open for 2% of the time, Pallas kernels for 8%

profile of v5, /device:TPU:1, one launch (start us, length us, event | category | flops | bytes accessed | tf_op | source)
XLA Modules:
  0.0 151.4 jit_solution(92679969826323771)
XLA Ops:
  0.6 1.4 broadcast_in_dim.23
  2.1 17.1 %all-to-all-start.1 = ((bf16[64,16,128]{2,1,0:T(8,128)(2,1)}), bf16[64,16,128]{2,1,0:T(8,128)(2,1)S(1)}, u32[]{:S(2)}, u32[]{:S(2)}) async-start(bf16[64,16,128]{2,1,0:T(8,128)(2,1)} %broadcast_in_dim.23), calls=%async_computation.1 | async-start | bytes 524288 | tf_op jit(solution)/shard_map/all_to_all | solution.py:33
  19.2 0.8 multiply_bitcast_fusion.cols
  20.0 12.3 %all-to-all-done.1 = bf16[64,16,128]{2,1,0:T(8,128)(2,1)S(1)} async-done(((bf16[64,16,128]{2,1,0:T(8,128)(2,1)}), bf16[64,16,128]{2,1,0:T(8,128)(2,1)S(1)}, u32[]{:S(2)}, u32[]{:S(2)}) %all-to-all-start.1) | async-done | bytes 262176 | tf_op jit(solution)/shard_map/all_to_all | solution.py:33
  32.3 1.4 broadcast_in_dim.20
  33.7 8.1 %all-to-all-start = ((bf16[64,16,128]{2,1,0:T(8,128)(2,1)}), bf16[64,16,128]{2,1,0:T(8,128)(2,1)S(1)}, u32[]{:S(2)}, u32[]{:S(2)}) async-start(bf16[64,16,128]{2,1,0:T(8,128)(2,1)} %broadcast_in_dim.20), calls=%async_computation | async-start | bytes 524288 | tf_op jit(solution)/shard_map/all_to_all | solution.py:33
  41.9 0.8 add_bitcast_fusion.depths
  42.7 0.8 reshape.59
  43.5 0.7 iota_compare_fusion
  44.3 2.9 %collective-permute-start = (bf16[1024,128]{1,0:T(8,128)(2,1)S(1)}, bf16[1024,128]{1,0:T(8,128)(2,1)S(1)}, u32[]{:S(2)}, u32[]{:S(2)}) collective-permute-start(bf16[1024,128]{1,0:T(8,128)(2,1)S(1)} %bitcast.15), channel_id=1, source_target_pairs={{0,4},{4,0},{1,5},{5,1},{2,6},{6,2},{3,7},{7,3},{8,12},{12,8},{9,1... | collective-permute-start | bytes 786440 | tf_op jit(solution)/shard_map/ppermute | solution.py:266
  47.2 0.1 broadcast_select_fusion.target
  47.3 8.5 %all-to-all-done = bf16[64,16,128]{2,1,0:T(8,128)(2,1)S(1)} async-done(((bf16[64,16,128]{2,1,0:T(8,128)(2,1)}), bf16[64,16,128]{2,1,0:T(8,128)(2,1)S(1)}, u32[]{:S(2)}, u32[]{:S(2)}) %all-to-all-start) | async-done | bytes 262176 | tf_op jit(solution)/shard_map/all_to_all | solution.py:33
  55.8 12.0 %shard_map.103.scaled = bf16[12288,256]{1,0:T(8,128)(2,1)} custom-call(s32[12288]{0:T(1024)S(1)} %multiply_bitcast_fusion.cols, bf16[12,8,128]{2,1,0:T(8,128)(2,1)} %bitcast.18, bf16[1024,128]{1,0:T(8,128)(2,1)S(1)} %bitcast.17), custom_call_target="tpu_custom_call" | custom-call | flops 1000000000 | bytes 1000000 | tf_op jit(solution)/shard_map/pallas_call | solution.py:182
  67.9 0.0 copy-start
  67.9 0.0 collective-permute-done.ranks_other
  67.9 11.6 %shard_map.104 = bf16[32,64,256]{2,1,0:T(8,128)(2,1)S(1)} custom-call(s32[12288]{0:T(1024)S(1)} %add_bitcast_fusion.depths, bf16[12288,256]{1,0:T(8,128)(2,1)} %shard_map.103.scaled, s32[32,3,128]{2,1,0:T(4,128)S(1)} %broadcast_select_fusion.target, bf16[1024,128]{1,0:T(8,128)(2,1)S(1)} %bitcast.16, bf16[1024,128]{1,0:T(8,128)(2,1)S(1)} %collective-permute-done.ranks_other), custom_call_target="tpu_custom_call" | custom-call | flops 1000000000 | bytes 1000000 | tf_op jit(solution)/shard_map/pallas_call | solution.py:182
  79.6 7.6 %all_to_all.40 = bf16[32,64,256]{2,1,0:T(8,128)(2,1)S(1)} all-to-all(bf16[32,64,256]{2,1,0:T(8,128)(2,1)S(1)} %shard_map.104), channel_id=1, replica_groups=mesh['ia'=16,'yl'=4,'co'=2,'ka'=4] {'co'}, dimensions={0} | all-to-all | bytes 2097152 | tf_op jit(solution)/shard_map/all_to_all | solution.py:33
  87.1 0.1 shard_map.105
  87.3 19.7 %all_to_all.41.arrived = bf16[16,64,256]{2,1,0:T(8,128)(2,1)S(1)} all-to-all(bf16[16,64,256]{2,1,0:T(8,128)(2,1)S(1)} %shard_map.105), channel_id=1, replica_groups=mesh['ia'=16,'yl'=4,'co'=2,'ka'=4] {'yl','ka'}, dimensions={0} | all-to-all | bytes 1048576 | tf_op jit(solution)/shard_map/all_to_all | solution.py:33
  106.9 0.0 copy-done
  106.9 1.1 shard_map.106
  108.0 10.3 %all_to_all.42.arrived = bf16[8,32,256]{2,1,0:T(8,128)(2,1)S(1)} all-to-all(bf16[8,32,256]{2,1,0:T(8,128)(2,1)S(1)} %get-tuple-element.7), channel_id=1, replica_groups=mesh['ia'=16,'yl'=4,'co'=2,'ka'=4] {'co','ka'}, dimensions={0} | all-to-all | bytes 262144 | tf_op jit(solution)/shard_map/all_to_all | solution.py:33
  118.4 7.2 %all_to_all.43.arrived = bf16[4,32,256]{2,1,0:T(8,128)(2,1)S(1)} all-to-all(bf16[4,32,256]{2,1,0:T(8,128)(2,1)S(1)} %shard_map.107), channel_id=1, replica_groups=mesh['ia'=16,'yl'=4,'co'=2,'ka'=4] {'yl'}, dimensions={0} | all-to-all | bytes 131072 | tf_op jit(solution)/shard_map/all_to_all | solution.py:33
  125.6 14.1 %all_to_all.44.arrived = bf16[16,32,256]{2,1,0:T(8,128)(2,1)S(1)} all-to-all(bf16[16,32,256]{2,1,0:T(8,128)(2,1)S(1)} %shard_map.108), channel_id=1, replica_groups=mesh['ia'=16,'yl'=4,'co'=2,'ka'=4] {'ia'}, dimensions={0} | all-to-all | bytes 524288 | tf_op jit(solution)/shard_map/all_to_all | solution.py:33
  139.8 10.9 %all_to_all.45 = bf16[8,32,256]{2,1,0:T(8,128)(2,1)S(1)} all-to-all(bf16[8,32,256]{2,1,0:T(8,128)(2,1)S(1)} %shard_map.109), channel_id=1, replica_groups=mesh['ia'=16,'yl'=4,'co'=2,'ka'=4] {'co','ka'}, dimensions={0} | all-to-all | bytes 262144 | tf_op jit(solution)/shard_map/all_to_all | solution.py:33
  150.7 0.7 bitcast_convert_fusion
  (3 shorter events, 0.1 us)
Async XLA Ops:
  2.1 30.2 %all-to-all-start.1 = ((bf16[64,16,128]{2,1,0:T(8,128)(2,1)}), bf16[64,16,128]{2,1,0:T(8,128)(2,1)S(1)}, u32[]{:S(2)}, u32[]{:S(2)}) async-start(bf16[64,16,128]{2,1,0:T(8,128)(2,1)} %broadcast_in_dim.23), calls=%async_computation.1 | async-start | bytes 524288 | tf_op jit(solution)/shard_map/all_to_all | solution.py:33
  33.7 22.1 %all-to-all-start = ((bf16[64,16,128]{2,1,0:T(8,128)(2,1)}), bf16[64,16,128]{2,1,0:T(8,128)(2,1)S(1)}, u32[]{:S(2)}, u32[]{:S(2)}) async-start(bf16[64,16,128]{2,1,0:T(8,128)(2,1)} %broadcast_in_dim.20), calls=%async_computation | async-start | bytes 524288 | tf_op jit(solution)/shard_map/all_to_all | solution.py:33
  44.3 23.6 %collective-permute-start = (bf16[1024,128]{1,0:T(8,128)(2,1)S(1)}, bf16[1024,128]{1,0:T(8,128)(2,1)S(1)}, u32[]{:S(2)}, u32[]{:S(2)}) collective-permute-start(bf16[1024,128]{1,0:T(8,128)(2,1)S(1)} %bitcast.15), channel_id=1, source_target_pairs={{0,4},{4,0},{1,5},{5,1},{2,6},{6,2},{3,7},{7,3},{8,12},{12,8},{9,1... | collective-permute-start | bytes 786440 | tf_op jit(solution)/shard_map/ppermute | solution.py:266
  67.9 39.1 %copy-start = (f32[16,256]{1,0:T(8,128)S(1)}, f32[16,256]{1,0:T(8,128)}, u32[]{:S(2)}) copy-start(f32[16,256]{1,0:T(8,128)} %proj.1) | copy-start | bytes 49156
